TPU v7x, 32 devices: a whole 2x2x4 slice. The times are simulated.
32 devices in a mesh: groups: 2 (over x), dp: 16 (over z, y, core).
Axes of the slice: x: 2, y: 2, z: 4, core: 2. Of those that a mesh axis runs over, the one named last changes fastest.
Arguments:
- queries: bfloat16 [24576, 4096], P(('groups', 'dp')), parts along dimension 0, may hold values from -120 to 120
- keys: bfloat16 [24576, 512], P(('groups', 'dp')), parts along dimension 0, may hold values from -6 to 6
- values: bfloat16 [24576, 512], P(('groups', 'dp')), parts along dimension 0, may hold values from -6 to 6
- block_counts: int32 [32], P(('groups', 'dp')), parts along dimension 0, may hold values from 0 to 6, as said below
- segment_ids: int32 [8192], P(('groups', 'dp')), parts along dimension 0, may hold values from 0 to 7, never falling along the last dimension, each value on 1 to 1024 neighbouring positions
- reward_dir: float32 [4096], replicated, may hold values from -4 to 4
Outputs:
- attn_out: bfloat16 [8192, 4096], P(('groups', 'dp')), parts along dimension 0
- rewards: float32 [16], P('groups'), parts along dimension 0
There are 2 independent parts, one for each index of `groups`. A program takes and returns all parts, laid end to end along the dimension named above; an argument that names none is the same for every part. Nothing has to cross between parts.
Inputs may be any that keep to these rules, and one draw needn't show every extreme that they name: `block_counts`: the counts sum to 2 times the number of ranks; for each rank s the counts of the ranks before s sum to between (2 * s - 2) and (2 * s + 2); some rank holds 6. `segment_ids`: positions never fall in segment number, each of the 8 responses holds 1 to 1024 positions.
All inputs are finite; a program needn't handle non-finite values.
Results may differ from a plain program's by a relative error of at most 0.0039.
The roundings to bfloat16 on the way count: a program that leaves them out, or rounds other values in their place, can miss the bound.
Values may be sent and summed in bfloat16 or wider, within the bound.
No kernel may reach another device: no remote copies, remote signals or barrier semaphores. Data moves between devices by JAX's collectives and lax.ppermute only.
A program may use at most 128 MiB of HBM per device.

v0:
```python
import jax
import jax.numpy as jnp
from jax import lax
from jax.sharding import PartitionSpec as P

D_HEAD = 128
HEADS = 32
KV_HEADS = 4
BLOCK = 128
RECV = 2
REACH = 4


def prefix_2(part, axis, combine, identity):
    place = lax.axis_index(axis)
    gathered = jax.tree.map(lambda a: lax.all_gather(a, axis), part)
    state = jax.tree.map(lambda a, e: jnp.zeros_like(a) + jnp.asarray(e, a.dtype), part, identity)

    def one(hop, state):
        return combine(
            state, jax.tree.map(lambda a: lax.dynamic_index_in_dim(a, hop, 0, False), gathered)
        )

    return lax.fori_loop(0, place, one, state)


def shifted(block, axis, distance):
    devices = range(lax.axis_size(axis))
    route = [(i - distance, i) for i in devices if i - distance in devices]
    return lax.ppermute(block, axis, route)


def shortened(shard):
    return jax.tree.map(lambda a: a.astype(jnp.bfloat16) if a.dtype == jnp.float32 else a, shard)


def attend(query_rows, key_window, value_window, allowed):
    per_group = HEADS // KV_HEADS
    row_count = query_rows.shape[0]
    score_scale = D_HEAD ** (-0.5)
    grouped = query_rows.reshape(row_count, KV_HEADS, per_group, D_HEAD)
    key_heads = key_window.reshape(-1, KV_HEADS, D_HEAD)
    value_heads = value_window.reshape(-1, KV_HEADS, D_HEAD)
    head_outs = []
    for head_index in range(KV_HEADS):
        query_head = grouped[:, head_index].reshape(row_count * per_group, D_HEAD)
        logits = (
            jnp.dot(query_head, key_heads[:, head_index].T, preferred_element_type=jnp.float32)
            * score_scale
        )
        logits = logits.reshape(row_count, per_group, -1)
        logits = jnp.where(allowed[:, None, :], logits, -1e30)
        row_max = jnp.max(logits, axis=-1, keepdims=True)
        raised = jnp.exp(logits - row_max)
        totals = jnp.sum(raised, axis=-1)
        soft_weights = raised.astype(jnp.bfloat16).reshape(row_count * per_group, -1)
        head_out = jnp.dot(
            soft_weights, value_heads[:, head_index], preferred_element_type=jnp.float32
        )
        head_out = head_out.reshape(row_count, per_group, D_HEAD) / totals[..., None]
        head_outs.append(head_out.astype(jnp.bfloat16))
    return jnp.stack(head_outs, axis=1).reshape(row_count, HEADS * D_HEAD)


def combine_all(earlier, later):
    count_a, first_a, last_a, start_a = earlier
    count_b, first_b, last_b, start_b = later
    joined = (first_b == last_b) & (last_a == first_b)
    empty_b = last_b < 0
    return (
        count_a + count_b,
        jnp.where(first_a < 0, first_b, first_a),
        jnp.where(empty_b, last_a, last_b),
        jnp.where(empty_b | joined, start_a, start_b),
    )


def shards(queries, keys, values, block_counts, segment_ids, reward_dir):
    row_count = segment_ids.shape[0]
    capacity = queries.shape[0] // BLOCK
    own_rank = lax.axis_index("dp")
    own_count = block_counts[0]
    positions = jnp.arange(row_count, dtype=jnp.int32)
    base_row = own_rank * row_count
    changed = jnp.concatenate([jnp.ones((1,), bool), segment_ids[1:] != segment_ids[:-1]])
    local_start = lax.cummax(jnp.where(changed, positions, 0), axis=0)
    summary = (
        block_counts,
        segment_ids[0:1],
        segment_ids[row_count - 1 : row_count],
        base_row + local_start[row_count - 1 : row_count],
    )
    neutral = (
        jnp.zeros((1,), jnp.int32),
        jnp.full((1,), -1, jnp.int32),
        jnp.full((1,), -1, jnp.int32),
        jnp.zeros((1,), jnp.int32),
    )
    prefix = prefix_2(summary, "dp", combine_all, neutral)
    offset = prefix[0][0]
    starts = jnp.where(segment_ids == prefix[2][0], prefix[3][0], base_row + local_start)
    following = shifted(segment_ids[0:1] + 1, "dp", -1)[0] - 1
    next_ids = jnp.concatenate([segment_ids[1:], following[None]])
    is_last = segment_ids != next_ids

    def outgoing(members, distance):
        first_pick = (own_rank + distance) * RECV - offset
        picks = first_pick + jnp.arange(RECV, dtype=jnp.int32)
        usable = (picks >= 0) & (picks < own_count)
        bounded = jnp.clip(picks, 0, capacity - 1)
        result = []
        for member in members:
            blocks = member.reshape(capacity, BLOCK, member.shape[1])
            chosen = jnp.take(blocks, bounded, axis=0)
            kept = jnp.where(usable[:, None, None], chosen, jnp.zeros_like(chosen))
            result.append(kept.reshape(row_count, member.shape[1]))
        return tuple(result)

    members = (queries, keys, values)
    arranged = outgoing(members, 0)
    for distance in (1, -1):
        parts = outgoing(members, distance)
        arrived = jax.tree.map(
            lambda part, own: part.astype(own.dtype),
            shifted(shortened(parts), "dp", distance),
            parts,
        )
        arranged = tuple((held + extra for held, extra in zip(arranged, arrived)))
    query_rows, key_rows, value_rows = arranged
    earlier = []
    carried = (key_rows, value_rows)
    for hop_index in range(REACH):
        carried = shifted((carried[0], carried[1]), "dp", 1)
        earlier.append(carried)
    earlier = earlier[::-1]
    key_window = jnp.concatenate([piece[0] for piece in earlier] + [key_rows], axis=0)
    value_window = jnp.concatenate([piece[1] for piece in earlier] + [value_rows], axis=0)
    key_window, value_window = (key_window, value_window)
    reach_rows = REACH * row_count
    key_pos = base_row - reach_rows + jnp.arange(reach_rows + row_count, dtype=jnp.int32)
    query_pos = base_row + positions
    allowed = (key_pos[None, :] >= starts[:, None]) & (key_pos[None, :] <= query_pos[:, None])
    attn_out = attend(query_rows, key_window, value_window, allowed)
    token_score = jnp.dot(attn_out.astype(jnp.float32), reward_dir, precision=lax.Precision.HIGHEST)
    response_count = lax.axis_size("dp") * 2 // REACH
    matches = (
        segment_ids[:, None] == jnp.arange(response_count, dtype=jnp.int32)[None, :]
    ) & is_last[:, None]
    partial_rewards = jnp.sum(jnp.where(matches, token_score[:, None], 0.0), axis=0)
    rewards = lax.psum(partial_rewards, "dp")
    return (attn_out, rewards)


def solution(mesh):
    return jax.shard_map(
        shards,
        mesh=mesh,
        in_specs=(
            P(("groups", "dp"), None),
            P(("groups", "dp"), None),
            P(("groups", "dp"), None),
            P(("groups", "dp")),
            P(("groups", "dp")),
            P(),
        ),
        out_specs=(P(("groups", "dp"), None), P("groups")),
        check_vma=False,
    )
```

profile of v0, /device:TPU:0, one launch (start us, length us, event | category | flops | bytes accessed | tf_op | source)
XLA Modules:
  0.0 308.4 jit_solution(2750992244555226999)
XLA Ops:
  2.0 1.9 fusion.63
  11.2 15.8 %all-reduce.4 = (s32[16]{0:T(128)S(1)}, s32[16]{0:T(128)S(1)}, s32[16]{0:T(128)S(1)}, s32[16]{0:T(128)S(1)}) all-reduce(s32[16]{0:T(128)S(1)} %dynamic-update-slice, s32[16]{0:T(128)S(1)} %slice_dynamic-update-slice_fusion, s32[16]{0:T(128)S(1)} %get-tuple-element.116, ...), channel_id=2, replica_groups=mesh['groups'=2,'dp'=16] {'dp'}, use_global_device_ids=true, to_apply=%add | all-reduce | flops 64 | bytes 512
  30.3 5.7 %collective-permute-start.2 = (bf16[256,512]{0,1:T(8,128)(2,1)}, bf16[256,512]{0,1:T(8,128)(2,1)}, u32[]{:S(2)}, u32[]{:S(2)}) collective-permute-start(bf16[256,512]{0,1:T(8,128)(2,1)} %copy.48), channel_id=1, source_target_pairs={{0,1},{1,2},{2,3},{3,4},{4,5},{5,6},{6,7},{7,8},{8,9},{9,10},{10,1... | collective-permute-start | bytes 786440 | tf_op jit(solution)/shard_map/ppermute | solution.py:30
  36.2 11.8 %collective-permute-start.8 = (bf16[256,512]{0,1:T(8,128)(2,1)S(1)}, bf16[256,512]{0,1:T(8,128)(2,1)}, u32[]{:S(2)}, u32[]{:S(2)}) collective-permute-start(bf16[256,512]{0,1:T(8,128)(2,1)S(1)} %copy.52), channel_id=1, source_target_pairs={{0,1},{1,2},{2,3},{3,4},{4,5},{5,6},{6,7},{7,8},{8,9},{9,10},{10,1... | collective-permute-start | bytes 786440 | tf_op jit(solution)/shard_map/ppermute | solution.py:30
  54.8 3.5 %gather_fusion.2 = bf16[2,128,4096]{2,1,0:T(8,128)(2,1)S(1)} fusion(bf16[6,128,4096]{2,1,0:T(8,128)(2,1)} %bitcast.181, s32[1024]{0:T(1024)S(1)} %get-tuple-element.133), kind=kCustom, calls=%fused_computation.3.clone | custom fusion | bytes 4194312 | tf_op jit(solution)/shard_map/jit(_take)/gather | solution.py:114
  62.2 3.5 %gather_fusion.1 = bf16[2,128,4096]{2,1,0:T(8,128)(2,1)S(1)} fusion(bf16[6,128,4096]{2,1,0:T(8,128)(2,1)} %bitcast.182, s32[1024]{0:T(1024)S(1)} %get-tuple-element.134), kind=kCustom, calls=%fused_computation.2.clone | custom fusion | bytes 4194312 | tf_op jit(solution)/shard_map/jit(_take)/gather | solution.py:114
  68.3 7.0 %collective-permute-start.10 = (bf16[256,512]{0,1:T(8,128)(2,1)S(1)}, bf16[256,512]{0,1:T(8,128)(2,1)S(1)}, u32[]{:S(2)}, u32[]{:S(2)}) collective-permute-start(bf16[256,512]{0,1:T(8,128)(2,1)S(1)} %add_add_fusion), channel_id=1, source_target_pairs={{0,1},{1,2},{2,3},{3,4},{4,5},{5,6},{6,7},{7,8},{8,9},{9,10},{10,1... | collective-permute-start | bytes 786440 | tf_op jit(solution)/shard_map/ppermute | solution.py:30
  76.9 3.5 %gather_fusion = bf16[2,128,4096]{2,1,0:T(8,128)(2,1)S(1)} fusion(bf16[6,128,4096]{2,1,0:T(8,128)(2,1)} %bitcast.183, s32[1024]{0:T(1024)S(1)} %pad_clamp_fusion.2), kind=kCustom, calls=%fused_computation.clone | custom fusion | bytes 4194312 | tf_op jit(solution)/shard_map/jit(_take)/gather | solution.py:114
  80.5 12.0 %collective-permute-start = (bf16[256,4096]{1,0:T(8,128)(2,1)}, bf16[256,4096]{1,0:T(8,128)(2,1)}, u32[]{:S(2)}, u32[]{:S(2)}) collective-permute-start(bf16[256,4096]{1,0:T(8,128)(2,1)} %bitcast.185), channel_id=1, source_target_pairs={{0,1},{1,2},{2,3},{3,4},{4,5},{5,6},{6,7},{7,8},{8,9},{9,10},{10,1... | collective-permute-start | bytes 6291464 | tf_op jit(solution)/shard_map/ppermute | solution.py:30
  93.5 4.9 %collective-permute-start.4 = (bf16[256,512]{0,1:T(8,128)(2,1)S(1)}, bf16[256,512]{0,1:T(8,128)(2,1)S(1)}, u32[]{:S(2)}, u32[]{:S(2)}) collective-permute-start(bf16[256,512]{0,1:T(8,128)(2,1)S(1)} %add_add_fusion.1), channel_id=1, source_target_pairs={{0,1},{1,2},{2,3},{3,4},{4,5},{5,6},{6,7},{7,8},{8,9},{9,10},{10,1... | collective-permute-start | bytes 786440 | tf_op jit(solution)/shard_map/ppermute | solution.py:30
  98.5 10.7 %collective-permute-start.11 = (bf16[256,512]{0,1:T(8,128)(2,1)S(1)}, bf16[256,512]{0,1:T(8,128)(2,1)S(1)}, u32[]{:S(2)}, u32[]{:S(2)}) collective-permute-start(bf16[256,512]{0,1:T(8,128)(2,1)S(1)} %collective-permute-done.10), channel_id=1, source_target_pairs={{0,1},{1,2},{2,3},{3,4},{4,5},{5,6},{6,7},{7,8},{8,9},{9,10},{10,1... | collective-permute-start | bytes 786440 | tf_op jit(solution)/shard_map/ppermute | solution.py:30
  110.8 32.0 %collective-permute-start.5 = (bf16[256,512]{0,1:T(8,128)(2,1)S(1)}, bf16[256,512]{0,1:T(8,128)(2,1)S(1)}, u32[]{:S(2)}, u32[]{:S(2)}) collective-permute-start(bf16[256,512]{0,1:T(8,128)(2,1)S(1)} %collective-permute-done.4), channel_id=1, source_target_pairs={{0,1},{1,2},{2,3},{3,4},{4,5},{5,6},{6,7},{7,8},{8,9},{9,10},{10,1... | collective-permute-start | bytes 786440 | tf_op jit(solution)/shard_map/ppermute | solution.py:30
  142.9 4.4 %collective-permute-start.12 = (bf16[256,512]{0,1:T(8,128)(2,1)S(1)}, bf16[256,512]{0,1:T(8,128)(2,1)S(1)}, u32[]{:S(2)}, u32[]{:S(2)}) collective-permute-start(bf16[256,512]{0,1:T(8,128)(2,1)S(1)} %collective-permute-done.11), channel_id=1, source_target_pairs={{0,1},{1,2},{2,3},{3,4},{4,5},{5,6},{6,7},{7,8},{8,9},{9,10},{10,1... | collective-permute-start | bytes 786440 | tf_op jit(solution)/shard_map/ppermute | solution.py:30
  147.3 3.2 %collective-permute-start.6 = (bf16[256,512]{0,1:T(8,128)(2,1)S(1)}, bf16[256,512]{0,1:T(8,128)(2,1)S(1)}, u32[]{:S(2)}, u32[]{:S(2)}) collective-permute-start(bf16[256,512]{0,1:T(8,128)(2,1)S(1)} %collective-permute-done.5), channel_id=1, source_target_pairs={{0,1},{1,2},{2,3},{3,4},{4,5},{5,6},{6,7},{7,8},{8,9},{9,10},{10,1... | collective-permute-start | bytes 786440 | tf_op jit(solution)/shard_map/ppermute | solution.py:30
  150.5 4.4 %collective-permute-start.13 = (bf16[256,512]{0,1:T(8,128)(2,1)S(1)}, bf16[256,512]{0,1:T(8,128)(2,1)S(1)}, u32[]{:S(2)}, u32[]{:S(2)}) collective-permute-start(bf16[256,512]{0,1:T(8,128)(2,1)S(1)} %collective-permute-done.12), channel_id=1, source_target_pairs={{0,1},{1,2},{2,3},{3,4},{4,5},{5,6},{6,7},{7,8},{8,9},{9,10},{10,1... | collective-permute-start | bytes 786440 | tf_op jit(solution)/shard_map/ppermute | solution.py:30
  156.1 21.6 %collective-permute-start.7 = (bf16[256,512]{0,1:T(8,128)(2,1)S(1)}, bf16[256,512]{0,1:T(8,128)(2,1)S(1)}, u32[]{:S(2)}, u32[]{:S(2)}) collective-permute-start(bf16[256,512]{0,1:T(8,128)(2,1)S(1)} %collective-permute-done.6), channel_id=1, source_target_pairs={{0,1},{1,2},{2,3},{3,4},{4,5},{5,6},{6,7},{7,8},{8,9},{9,10},{10,1... | collective-permute-start | bytes 786440 | tf_op jit(solution)/shard_map/ppermute | solution.py:30
  179.5 2.5 fusion.24
  182.5 2.7 fusion.64
  185.1 5.6 %fusion.65 = (f32[2048]{0:T(1024)S(1)}, f32[2048,1280]{1,0:T(8,128)}) fusion(bf16[1280,4,128]{0,2,1:T(8,128)(2,1)S(1)} %bitcast.187, bf16[256,4,8,128]{3,2,1,0:T(8,128)(2,1)S(1)} %bitcast.177, pred[256,1280]{1,0:T(8,128)(4,1)S(1)} %compare_and_fusion), kind=kOutput, calls=%fused_computation.122 | convolution fusion | flops 678950912 | bytes 11673600 | tf_op jit(solution)/shard_map/dot_general | solution.py:48
  190.8 5.3 %fusion.66 = (f32[2048]{0:T(1024)S(1)}, f32[2048,1280]{1,0:T(8,128)}) fusion(bf16[1280,4,128]{0,2,1:T(8,128)(2,1)S(1)} %bitcast.188, bf16[256,4,8,128]{3,2,1,0:T(8,128)(2,1)S(1)} %bitcast.178, pred[256,1280]{1,0:T(8,128)(4,1)S(1)} %compare_and_fusion), kind=kOutput, calls=%fused_computation.123 | convolution fusion | flops 678950912 | bytes 11673600 | tf_op jit(solution)/shard_map/dot_general | solution.py:48
  196.1 5.1 %fusion.67 = (f32[2048]{0:T(1024)S(1)}, f32[2048,1280]{1,0:T(8,128)}) fusion(bf16[1280,4,128]{0,2,1:T(8,128)(2,1)S(1)} %bitcast.189, bf16[256,4,8,128]{3,2,1,0:T(8,128)(2,1)S(1)} %bitcast.179, pred[256,1280]{1,0:T(8,128)(4,1)S(1)} %compare_and_fusion), kind=kOutput, calls=%fused_computation.124 | convolution fusion | flops 678950912 | bytes 11673600 | tf_op jit(solution)/shard_map/dot_general | solution.py:48
  201.2 1.8 fusion.6
  203.1 5.7 %fusion.4 = f32[2048]{0:T(1024)S(1)} fusion(f32[2048,1280]{1,0:T(8,128)} %get-tuple-element.126, f32[2048]{0:T(1024)S(1)} %get-tuple-element.125), kind=kLoop, calls=%fused_computation.25 | loop fusion | flops 5240832 | bytes 10502144 | tf_op jit(solution)/shard_map/reduce_sum | solution.py:55
  208.9 6.0 %fusion.58 = bf16[256,1,8,128]{3,2,0,1:T(8,128)(2,1)S(1)} fusion(f32[2048,1280]{1,0:T(8,128)} %copy-done.2, f32[2048]{0:T(1024)S(1)} %get-tuple-element.123, f32[256,8]{1,0:T(8,128)S(1)} %div.49, bf16[1280,4,128]{0,2,1:T(8,128)(2,1)S(1)} %bitcast.199), kind=kOutput, calls=%fused_computation.59 | convolution fusion | flops 676855808 | bytes 11476992 | tf_op jit(solution)/shard_map/dot_general | solution.py:57
  214.9 6.0 %fusion.49 = bf16[256,1,8,128]{3,2,0,1:T(8,128)(2,1)S(1)} fusion(f32[2048,1280]{1,0:T(8,128)} %get-tuple-element.126, f32[2048]{0:T(1024)S(1)} %get-tuple-element.125, f32[256,8]{1,0:T(8,128)S(1)} %div.46, bf16[1280,4,128]{0,2,1:T(8,128)(2,1)S(1)} %bitcast.200), kind=kOutput, calls=%fused_computation.56 | convolution fusion | flops 676855808 | bytes 11476992 | tf_op jit(solution)/shard_map/dot_general | solution.py:57
  220.9 1.8 fusion.2
  222.8 5.8 %fusion.40 = bf16[256,1,8,128]{3,2,0,1:T(8,128)(2,1)S(1)} fusion(f32[2048,1280]{1,0:T(8,128)} %get-tuple-element.128, f32[2048]{0:T(1024)S(1)} %get-tuple-element.127, f32[256,8]{1,0:T(8,128)S(1)} %div.43, bf16[1280,4,128]{0,2,1:T(8,128)(2,1)S(1)} %bitcast.201), kind=kOutput, calls=%fused_computation.53 | convolution fusion | flops 676855808 | bytes 11476992 | tf_op jit(solution)/shard_map/dot_general | solution.py:57
  228.6 5.9 %fusion = f32[2048]{0:T(1024)S(1)} fusion(f32[2048,1280]{1,0:T(8,128)} %get-tuple-element.130, f32[2048]{0:T(1024)S(1)} %get-tuple-element.129), kind=kLoop, calls=%fused_computation.21 | loop fusion | flops 5240832 | bytes 10502144 | tf_op jit(solution)/shard_map/reduce_sum | solution.py:55
  234.7 5.8 %fusion.31 = bf16[256,1,8,128]{3,2,0,1:T(8,128)(2,1)S(1)} fusion(f32[2048,1280]{1,0:T(8,128)} %get-tuple-element.130, f32[2048]{0:T(1024)S(1)} %get-tuple-element.129, f32[256,8]{1,0:T(8,128)S(1)} %div.40, bf16[1280,4,128]{0,2,1:T(8,128)(2,1)S(1)} %bitcast.202), kind=kOutput, calls=%fused_computation.50 | convolution fusion | flops 676855808 | bytes 11476992 | tf_op jit(solution)/shard_map/dot_general | solution.py:57
  242.1 3.0 copy.62
  246.1 2.9 copy.63
  249.0 59.4 %psum.7 = f32[8]{0:T(128)} all-reduce(f32[8]{0:T(128)S(1)} %select_reduce_fusion), channel_id=1, replica_groups=mesh['groups'=2,'dp'=16] {'dp'}, use_global_device_ids=true, to_apply=%region_13.16 | all-reduce | flops 8 | bytes 64 | tf_op jit(solution)/shard_map/psum | solution.py:150
  (116 shorter events, 34.1 us)
Async XLA Ops:
  0.6 26.4 %copy-start = (bf16[768,512]{1,0:T(8,128)(2,1)S(1)}, bf16[768,512]{1,0:T(8,128)(2,1)}, u32[]{:S(2)}) copy-start(bf16[768,512]{1,0:T(8,128)(2,1)} %param.14) | copy-start | bytes 2359300
  4.5 150.8 %collective-permute-start.14 = (s32[1]{0:T(128)}, s32[1]{0:T(128)}, u32[]{:S(2)}, u32[]{:S(2)}) collective-permute-start(s32[1]{0:T(128)} %add.136), channel_id=1, source_target_pairs={{1,0},{2,1},{3,2},{4,3},{5,4},{6,5},{7,6},{8,7},{9,8},{10,9},{11,1... | collective-permute-start | bytes 20 | tf_op jit(solution)/shard_map/ppermute | solution.py:30
  30.3 50.2 %collective-permute-start.2 = (bf16[256,512]{0,1:T(8,128)(2,1)}, bf16[256,512]{0,1:T(8,128)(2,1)}, u32[]{:S(2)}, u32[]{:S(2)}) collective-permute-start(bf16[256,512]{0,1:T(8,128)(2,1)} %copy.48), channel_id=1, source_target_pairs={{0,1},{1,2},{2,3},{3,4},{4,5},{5,6},{6,7},{7,8},{8,9},{9,10},{10,1... | collective-permute-start | bytes 786440 | tf_op jit(solution)/shard_map/ppermute | solution.py:30
  36.2 29.7 %collective-permute-start.8 = (bf16[256,512]{0,1:T(8,128)(2,1)S(1)}, bf16[256,512]{0,1:T(8,128)(2,1)}, u32[]{:S(2)}, u32[]{:S(2)}) collective-permute-start(bf16[256,512]{0,1:T(8,128)(2,1)S(1)} %copy.52), channel_id=1, source_target_pairs={{0,1},{1,2},{2,3},{3,4},{4,5},{5,6},{6,7},{7,8},{8,9},{9,10},{10,1... | collective-permute-start | bytes 786440 | tf_op jit(solution)/shard_map/ppermute | solution.py:30
  51.3 41.2 %collective-permute-start.3 = (bf16[256,512]{0,1:T(8,128)(2,1)}, bf16[256,512]{0,1:T(8,128)(2,1)}, u32[]{:S(2)}, u32[]{:S(2)}) collective-permute-start(bf16[256,512]{0,1:T(8,128)(2,1)} %copy.50), channel_id=1, source_target_pairs={{1,0},{2,1},{3,2},{4,3},{5,4},{6,5},{7,6},{8,7},{9,8},{10,9},{11,1... | collective-permute-start | bytes 786440 | tf_op jit(solution)/shard_map/ppermute | solution.py:30
  53.4 13.8 %collective-permute-start.9 = (bf16[256,512]{0,1:T(8,128)(2,1)}, bf16[256,512]{0,1:T(8,128)(2,1)}, u32[]{:S(2)}, u32[]{:S(2)}) collective-permute-start(bf16[256,512]{0,1:T(8,128)(2,1)} %copy.54), channel_id=1, source_target_pairs={{1,0},{2,1},{3,2},{4,3},{5,4},{6,5},{7,6},{8,7},{9,8},{10,9},{11,1... | collective-permute-start | bytes 786440 | tf_op jit(solution)/shard_map/ppermute | solution.py:30
  65.9 113.2 %collective-permute-start.1 = (bf16[256,4096]{1,0:T(8,128)(2,1)}, bf16[256,4096]{1,0:T(8,128)(2,1)}, u32[]{:S(2)}, u32[]{:S(2)}) collective-permute-start(bf16[256,4096]{1,0:T(8,128)(2,1)} %bitcast.184), channel_id=1, source_target_pairs={{1,0},{2,1},{3,2},{4,3},{5,4},{6,5},{7,6},{8,7},{9,8},{10,9},{11,1... | collective-permute-start | bytes 6291464 | tf_op jit(solution)/shard_map/ppermute | solution.py:30
  68.3 30.2 %collective-permute-start.10 = (bf16[256,512]{0,1:T(8,128)(2,1)S(1)}, bf16[256,512]{0,1:T(8,128)(2,1)S(1)}, u32[]{:S(2)}, u32[]{:S(2)}) collective-permute-start(bf16[256,512]{0,1:T(8,128)(2,1)S(1)} %add_add_fusion), channel_id=1, source_target_pairs={{0,1},{1,2},{2,3},{3,4},{4,5},{5,6},{6,7},{7,8},{8,9},{9,10},{10,1... | collective-permute-start | bytes 786440 | tf_op jit(solution)/shard_map/ppermute | solution.py:30
  80.5 98.7 %collective-permute-start = (bf16[256,4096]{1,0:T(8,128)(2,1)}, bf16[256,4096]{1,0:T(8,128)(2,1)}, u32[]{:S(2)}, u32[]{:S(2)}) collective-permute-start(bf16[256,4096]{1,0:T(8,128)(2,1)} %bitcast.185), channel_id=1, source_target_pairs={{0,1},{1,2},{2,3},{3,4},{4,5},{5,6},{6,7},{7,8},{8,9},{9,10},{10,1... | collective-permute-start | bytes 6291464 | tf_op jit(solution)/shard_map/ppermute | solution.py:30
  93.5 53.7 %copy-start.9 = (s32[256]{0:T(256)S(1)}, s32[256]{0:T(256)}, u32[]{:S(2)}) copy-start(s32[256]{0:T(256)} %param.16) | copy-start | bytes 3076
  93.5 17.2 %collective-permute-start.4 = (bf16[256,512]{0,1:T(8,128)(2,1)S(1)}, bf16[256,512]{0,1:T(8,128)(2,1)S(1)}, u32[]{:S(2)}, u32[]{:S(2)}) collective-permute-start(bf16[256,512]{0,1:T(8,128)(2,1)S(1)} %add_add_fusion.1), channel_id=1, source_target_pairs={{0,1},{1,2},{2,3},{3,4},{4,5},{5,6},{6,7},{7,8},{8,9},{9,10},{10,1... | collective-permute-start | bytes 786440 | tf_op jit(solution)/shard_map/ppermute | solution.py:30
  98.5 44.4 %collective-permute-start.11 = (bf16[256,512]{0,1:T(8,128)(2,1)S(1)}, bf16[256,512]{0,1:T(8,128)(2,1)S(1)}, u32[]{:S(2)}, u32[]{:S(2)}) collective-permute-start(bf16[256,512]{0,1:T(8,128)(2,1)S(1)} %collective-permute-done.10), channel_id=1, source_target_pairs={{0,1},{1,2},{2,3},{3,4},{4,5},{5,6},{6,7},{7,8},{8,9},{9,10},{10,1... | collective-permute-start | bytes 786440 | tf_op jit(solution)/shard_map/ppermute | solution.py:30
  110.8 39.7 %copy-start.4 = (bf16[256,512]{0,1:T(8,128)(2,1)}, bf16[256,512]{0,1:T(8,128)(2,1)S(1)}, u32[]{:S(2)}) copy-start(bf16[256,512]{0,1:T(8,128)(2,1)S(1)} %collective-permute-done.4) | copy-start | bytes 786436
  110.8 36.5 %collective-permute-start.5 = (bf16[256,512]{0,1:T(8,128)(2,1)S(1)}, bf16[256,512]{0,1:T(8,128)(2,1)S(1)}, u32[]{:S(2)}, u32[]{:S(2)}) collective-permute-start(bf16[256,512]{0,1:T(8,128)(2,1)S(1)} %collective-permute-done.4), channel_id=1, source_target_pairs={{0,1},{1,2},{2,3},{3,4},{4,5},{5,6},{6,7},{7,8},{8,9},{9,10},{10,1... | collective-permute-start | bytes 786440 | tf_op jit(solution)/shard_map/ppermute | solution.py:30
  142.8 7.7 %copy-start.6 = (bf16[256,512]{0,1:T(8,128)(2,1)}, bf16[256,512]{0,1:T(8,128)(2,1)S(1)}, u32[]{:S(2)}) copy-start(bf16[256,512]{0,1:T(8,128)(2,1)S(1)} %collective-permute-done.11) | copy-start | bytes 786436
  142.9 7.7 %collective-permute-start.12 = (bf16[256,512]{0,1:T(8,128)(2,1)S(1)}, bf16[256,512]{0,1:T(8,128)(2,1)S(1)}, u32[]{:S(2)}, u32[]{:S(2)}) collective-permute-start(bf16[256,512]{0,1:T(8,128)(2,1)S(1)} %collective-permute-done.11), channel_id=1, source_target_pairs={{0,1},{1,2},{2,3},{3,4},{4,5},{5,6},{6,7},{7,8},{8,9},{9,10},{10,1... | collective-permute-start | bytes 786440 | tf_op jit(solution)/shard_map/ppermute | solution.py:30
  147.3 8.8 %collective-permute-start.6 = (bf16[256,512]{0,1:T(8,128)(2,1)S(1)}, bf16[256,512]{0,1:T(8,128)(2,1)S(1)}, u32[]{:S(2)}, u32[]{:S(2)}) collective-permute-start(bf16[256,512]{0,1:T(8,128)(2,1)S(1)} %collective-permute-done.5), channel_id=1, source_target_pairs={{0,1},{1,2},{2,3},{3,4},{4,5},{5,6},{6,7},{7,8},{8,9},{9,10},{10,1... | collective-permute-start | bytes 786440 | tf_op jit(solution)/shard_map/ppermute | solution.py:30
  150.5 27.2 %collective-permute-start.13 = (bf16[256,512]{0,1:T(8,128)(2,1)S(1)}, bf16[256,512]{0,1:T(8,128)(2,1)S(1)}, u32[]{:S(2)}, u32[]{:S(2)}) collective-permute-start(bf16[256,512]{0,1:T(8,128)(2,1)S(1)} %collective-permute-done.12), channel_id=1, source_target_pairs={{0,1},{1,2},{2,3},{3,4},{4,5},{5,6},{6,7},{7,8},{8,9},{9,10},{10,1... | collective-permute-start | bytes 786440 | tf_op jit(solution)/shard_map/ppermute | solution.py:30
  156.1 23.0 %copy-start.5 = (bf16[256,512]{0,1:T(8,128)(2,1)S(1)}, bf16[256,512]{0,1:T(8,128)(2,1)}, u32[]{:S(2)}) copy-start(bf16[256,512]{0,1:T(8,128)(2,1)} %copy-done.4) | copy-start | bytes 786436
  156.1 22.9 %collective-permute-start.7 = (bf16[256,512]{0,1:T(8,128)(2,1)S(1)}, bf16[256,512]{0,1:T(8,128)(2,1)S(1)}, u32[]{:S(2)}, u32[]{:S(2)}) collective-permute-start(bf16[256,512]{0,1:T(8,128)(2,1)S(1)} %collective-permute-done.6), channel_id=1, source_target_pairs={{0,1},{1,2},{2,3},{3,4},{4,5},{5,6},{6,7},{7,8},{8,9},{9,10},{10,1... | collective-permute-start | bytes 786440 | tf_op jit(solution)/shard_map/ppermute | solution.py:30
  177.8 1.7 copy-start.3
  179.0 35.9 %copy-start.7 = (bf16[1280,512]{0,1:T(8,128)(2,1)}, bf16[1280,512]{0,1:T(8,128)(2,1)S(1)}, u32[]{:S(2)}) copy-start(bf16[1280,512]{0,1:T(8,128)(2,1)S(1)} %constant_dynamic-update-slice_fusion.5) | copy-start | bytes 3932164
  185.1 16.1 %copy-start.2 = (f32[2048,1280]{1,0:T(8,128)}, f32[2048,1280]{1,0:T(8,128)S(1)}, u32[]{:S(2)}) copy-start(f32[2048,1280]{1,0:T(8,128)S(1)} %get-tuple-element.124) | copy-start | bytes 31457284
  208.9 12.0 %slice-start = ((s8[10485760]{0:T(1024)(128)(4,1)}), s8[4194304]{0:T(1024)(128)(4,1)S(1)}, s32[]{:S(2)}) async-start(s8[10485760]{0:T(1024)(128)(4,1)} %bitcast.172), calls=%async_computation | async-start | bytes 8388608
  208.9 12.0 %slice-start.1 = ((s8[10485760]{0:T(1024)(128)(4,1)}), s8[4194304]{0:T(1024)(128)(4,1)S(1)}, s32[]{:S(2)}) async-start(s8[10485760]{0:T(1024)(128)(4,1)} %bitcast.172), calls=%async_computation.1 | async-start | bytes 8388608
  214.9 6.0 %slice-start.2 = ((s8[10485760]{0:T(1024)(128)(4,1)}), s8[2097152]{0:T(1024)(128)(4,1)S(1)}, s32[]{:S(2)}) async-start(s8[10485760]{0:T(1024)(128)(4,1)} %bitcast.172), calls=%async_computation.2 | async-start | bytes 4194304
  220.9 1.9 copy-start.8
  242.1 3.0 copy-start.10
  246.0 62.4 %copy-start.1 = (bf16[768,512]{1,0:T(8,128)(2,1)S(1)}, bf16[768,512]{1,0:T(8,128)(2,1)}, u32[]{:S(2)}) copy-start(bf16[768,512]{1,0:T(8,128)(2,1)} %param.14) | copy-start | bytes 2359300
where the time goes:
time: 310 us; the launch traced here: 308 us
  starting transfers between devices  123 us (40%)
  blocking collectives  75.2 us (24%)
  matrix products  43.2 us (14%)
  local copies, waits for them, and re-layouts  34.3 us (11%)
  other arithmetic  29.4 us (9%)
  between operations  3.36 us (1%)
    ppermute x15, starting transfers between devices, shifted(): return lax.ppermute(block, axis, route)  123 us
    psum x1, blocking collectives, shards(): rewards = lax.psum(partial_rewards, 'dp')  59.4 us
    dot_general x4, matrix products, attend(): jnp.dot(soft_weights, value_heads[:, head_index], preferred_element_type=...  23.6 us
    dot_general x4, matrix products, attend(): jnp.dot(query_head, key_heads[:, head_index].T, preferred_element_type=jn...  18.7 us
    gather x9, local copies, waits for them, and re-layouts, outgoing(): chosen = jnp.take(blocks, bounded, axis=0)  17.2 us
    unnamed x1, blocking collectives  15.8 us
    reduce_sum x4, other arithmetic, attend(): totals = jnp.sum(raised, axis=-1)  15.1 us
    unnamed x45, local copies, waits for them, and re-layouts  8.63 us
  transfers between devices with their start and end apart: 15, of which 0 were waited for; matrix products, arithmetic and copies ran while one was open for 11% of the time, Pallas kernels for 0%

commit v1 on v0

v1 whole, which is shorter than its diff:
```python
import functools
import math

import jax
import jax.numpy as jnp
from jax import lax
from jax.experimental import pallas as pl
from jax.experimental.pallas import tpu as pltpu
from jax.sharding import PartitionSpec as P

D_HEAD = 128
HEADS = 32
KV_HEADS = 4
BLOCK = 128
RECV = 2
REACH = 4
PER_GROUP = HEADS // KV_HEADS
ROWS = RECV * BLOCK
PIECES = REACH + 1
KV_WIDTH = KV_HEADS * D_HEAD
WIDTH = HEADS * D_HEAD
CHUNK = PER_GROUP * D_HEAD
STACKED = PER_GROUP * BLOCK
PAIR = 2
MASKED = -1e30
WIDE = pltpu.CompilerParams(vmem_limit_bytes=58 * 1024 * 1024 + 256 * 1024)
SLIM = pltpu.CompilerParams(vmem_limit_bytes=28 * 1024 * 1024)
EXP2_SCALE = D_HEAD ** (-0.5) * math.log2(math.e)
SPLIT = ((0,), (1, 2), (3,))

SMEM = pl.BlockSpec(memory_space=pltpu.SMEM)
VMEM = pl.BlockSpec(memory_space=pltpu.VMEM)
HBM = pl.BlockSpec(memory_space=pltpu.HBM)


def shifted(block, axis, distance):
    devices = range(lax.axis_size(axis))
    route = [(i - distance, i) for i in devices if i - distance in devices]
    return lax.ppermute(block, axis, route)


def inner_pairs(block, ranks):
    return lax.ppermute(block, "dp", [(i, i ^ 1) for i in range(ranks)])


def outer_pairs(block, ranks):
    route = []
    for low in range(1, ranks - 1, 2):
        route += [(low, low + 1), (low + 1, low)]
    return lax.ppermute(block, "dp", route)


def block_rows(index):
    return pl.ds(pl.multiple_of(index * BLOCK, BLOCK), BLOCK)


def columns_of(heads):
    return pl.ds(heads[0] * CHUNK, len(heads) * CHUNK)


def transfer(copies):
    for copy in copies:
        copy.start()
    for copy in copies:
        copy.wait()


def end_rows(counts, place, capacity):
    tail = jnp.clip(counts[0] - RECV, 0, capacity - RECV) * BLOCK
    odd = lax.rem(place[0], 2) == 1
    outer = pl.multiple_of(jnp.where(odd, tail, 0), BLOCK)
    inner = pl.multiple_of(jnp.where(odd, 0, tail), BLOCK)
    return pl.ds(outer, ROWS), pl.ds(inner, ROWS)


def first_stage_kernel(capacity, counts, place, queries, keys, values, kv_outer, kv_inner, q_outer, sems):
    outer, inner = end_rows(counts, place, capacity)
    key_part, value_part = pl.ds(0, KV_WIDTH), pl.ds(KV_WIDTH, KV_WIDTH)
    transfer([
        pltpu.make_async_copy(keys.at[outer], kv_outer.at[:, key_part], sems.at[0]),
        pltpu.make_async_copy(values.at[outer], kv_outer.at[:, value_part], sems.at[1]),
        pltpu.make_async_copy(keys.at[inner], kv_inner.at[:, key_part], sems.at[2]),
        pltpu.make_async_copy(values.at[inner], kv_inner.at[:, value_part], sems.at[3]),
        pltpu.make_async_copy(queries.at[outer, columns_of(SPLIT[0])], q_outer, sems.at[4]),
    ])


def first_stage(counts, place, queries, keys, values):
    capacity = queries.shape[0] // BLOCK
    kv = jax.ShapeDtypeStruct((ROWS, 2 * KV_WIDTH), keys.dtype)
    q = jax.ShapeDtypeStruct((ROWS, len(SPLIT[0]) * CHUNK), queries.dtype)
    return pl.pallas_call(
        functools.partial(first_stage_kernel, capacity),
        out_shape=(kv, kv, q),
        in_specs=[SMEM, SMEM, HBM, HBM, HBM],
        out_specs=(VMEM, VMEM, VMEM),
        scratch_shapes=[pltpu.SemaphoreType.DMA((5,))],
        compiler_params=WIDE,
        name="first_stage",
    )(counts, place, queries, keys, values)


def second_stage_kernel(capacity, counts, place, queries, *rest):
    outs, sems = rest[:-1], rest[-1]
    outer, inner = end_rows(counts, place, capacity)
    copies = [
        pltpu.make_async_copy(queries.at[outer, columns_of(heads)], out, sems.at[i])
        for i, (heads, out) in enumerate(zip(SPLIT[1:], outs))
    ]
    copies.append(pltpu.make_async_copy(queries.at[inner], outs[-1], sems.at[len(SPLIT) - 1]))
    transfer(copies)


def second_stage(counts, place, queries):
    capacity = queries.shape[0] // BLOCK
    widths = [len(heads) * CHUNK for heads in SPLIT[1:]] + [WIDTH]
    return pl.pallas_call(
        functools.partial(second_stage_kernel, capacity),
        out_shape=tuple(jax.ShapeDtypeStruct((ROWS, width), queries.dtype) for width in widths),
        in_specs=[SMEM, SMEM, HBM],
        out_specs=(VMEM,) * len(widths),
        scratch_shapes=[pltpu.SemaphoreType.DMA((len(SPLIT),))],
        compiler_params=WIDE,
        name="second_stage",
    )(counts, place, queries)


def placement(info, place, responses, ranks):
    rank = place[0]
    before = lax.fori_loop(
        0, ranks, lambda s, t: t + jnp.where(s < rank, info[responses + s], 0), jnp.int32(0)
    )
    left_count = info[responses + jnp.maximum(rank - 1, 0)]
    return rank, before - rank * RECV, info[responses + rank], left_count


def pick(k, rank, excess, count, left_count, capacity):
    left_first = jnp.clip(left_count - RECV, 0, capacity - RECV)
    from_left = k < excess
    slot = k - excess
    is_own = jnp.logical_and(jnp.logical_not(from_left), slot < count)
    odd = lax.rem(rank, 2)
    left_kind, right_kind = jnp.where(odd == 1, 2, 0), jnp.where(odd == 1, 0, 2)
    kind = jnp.where(from_left, left_kind, jnp.where(is_own, 1, right_kind))
    index = jnp.where(
        from_left, left_count - excess + k - left_first, jnp.where(is_own, slot, slot - count)
    )
    limit = jnp.where(is_own, capacity - 1, RECV - 1)
    return kind, jnp.clip(index, 0, limit)


def pack_kernel(
    responses, ranks, capacity,
    info, place, queries, keys, values, outer, inner,
    out, q_own, sems,
):
    rank, excess, count, left_count = placement(info, place, responses, ranks)
    picks = [pick(k, rank, excess, count, left_count, capacity) for k in range(RECV)]
    jobs = []
    key_part, value_part = pl.ds(0, KV_WIDTH), pl.ds(KV_WIDTH, KV_WIDTH)
    for k, (kind, index) in enumerate(picks):
        rows = block_rows(index)
        into = pl.ds(k * BLOCK, BLOCK)
        mine = kind == 1
        jobs += [
            (mine, pltpu.make_async_copy(keys.at[rows], out.at[into, key_part], sems.at[k, 0])),
            (mine, pltpu.make_async_copy(values.at[rows], out.at[into, value_part], sems.at[k, 1])),
            (mine, pltpu.make_async_copy(queries.at[rows], q_own.at[into], sems.at[k, 2])),
        ]
    each(jobs, "start")

    for k, (kind, index) in enumerate(picks):
        for wanted, source in ((0, outer), (2, inner)):
            @pl.when(kind == wanted)
            def _(source=source, k=k, index=index):
                out[k * BLOCK:(k + 1) * BLOCK, :] = source[block_rows(index), :]
    each(jobs, "wait")


def pack(info, place, queries, keys, values, outer, inner, responses, ranks):
    capacity = keys.shape[0] // BLOCK
    return pl.pallas_call(
        functools.partial(pack_kernel, responses, ranks, capacity),
        out_shape=(
            jax.ShapeDtypeStruct((ROWS, 2 * KV_WIDTH), keys.dtype),
            jax.ShapeDtypeStruct((ROWS, WIDTH), queries.dtype),
        ),
        in_specs=[SMEM, SMEM, HBM, HBM, HBM, VMEM, VMEM],
        out_specs=(VMEM, VMEM),
        scratch_shapes=[
            pltpu.SemaphoreType.DMA((RECV, 3)),
        ],
        compiler_params=WIDE,
        name="pack",
    )(info, place, queries, keys, values, outer, inner)


def fill_window(rank, window, head, lowest, kbuf, vbuf):
    own, two, four, sib_own, sib_two, sib_four = window
    odd = lax.rem(rank, 2) == 1
    even = jnp.logical_not(odd)
    sources = ((None, own, 4), (odd, sib_own, 3), (even, sib_two, 3), (None, two, 2),
               (odd, sib_two, 1), (even, sib_four, 1), (None, four, 0))
    for condition, source, piece in sources:
        needed = lowest <= piece
        if condition is not None:
            needed = jnp.logical_and(needed, condition)

        @pl.when(needed)
        def _(source=source, piece=piece):
            kbuf[piece] = source[:, head * D_HEAD:(head + 1) * D_HEAD]
            vbuf[piece] = source[:, KV_WIDTH + head * D_HEAD:KV_WIDTH + (head + 1) * D_HEAD]


def each(jobs, action):
    for condition, copy in jobs:
        if condition is None:
            getattr(copy, action)()
        else:
            pl.when(condition)(getattr(copy, action))


def attend_kernel(
    responses, ranks, capacity, heads, earlier, rewards,
    info, place, q_own, q_outer, q_inner, own, two, four, sib_own, sib_two, sib_four,
    reward_dir, out, score, kbuf, vbuf, qbuf, obuf, sbuf, mbuf, lbuf, abuf, o_sems,
):
    rank, excess, count, left_count = placement(info, place, responses, ranks)
    columns = slice(heads[0] * CHUNK, (heads[-1] + 1) * CHUNK)
    for k in range(RECV):
        kind, index = pick(k, rank, excess, count, left_count, capacity)

        @pl.when(kind == 0)
        def _(k=k, index=index):
            qbuf[k] = q_outer[block_rows(index), :]

        @pl.when(kind == 1)
        def _(k=k):
            qbuf[k] = q_own[k * BLOCK:(k + 1) * BLOCK, columns]

        @pl.when(kind == 2)
        def _(k=k, index=index):
            qbuf[k] = q_inner[block_rows(index), columns]

    window = (own, two, four, sib_own, sib_two, sib_four)
    window_base = (rank - REACH) * ROWS
    first = rank * ROWS
    row_iota = lax.broadcasted_iota(jnp.int32, (ROWS, D_HEAD), 0)
    lane_iota = lax.broadcasted_iota(jnp.int32, (BLOCK, D_HEAD), 1)
    rows_at = row_iota + first

    def widen(r, carry):
        begin, begins = carry
        start = info[r]
        begin = jnp.where(start <= first, jnp.maximum(begin, start), begin)
        begins = jnp.where(rows_at >= start, jnp.maximum(begins, start), begins)
        return begin, begins

    begin, begins = lax.fori_loop(
        0, responses, widen, (jnp.int32(0), jnp.zeros((ROWS, D_HEAD), jnp.int32))
    )
    lowest = jnp.clip((begin - window_base) // ROWS, 0, REACH)

    stores = []
    score[...] = jnp.zeros_like(score)
    for at, head in enumerate(heads):
        fill_window(rank, window, head, lowest, kbuf, vbuf)
        mbuf[...] = jnp.full_like(mbuf, MASKED)

        def score_tile(p, _):
            base = window_base + p * ROWS
            key_tile = kbuf[p]
            for k in range(RECV):
                block = slice(k * BLOCK, (k + 1) * BLOCK)
                masks = []
                for half in range(2):
                    key_at = lane_iota + (base + half * D_HEAD)
                    masks.append(jnp.logical_and(key_at >= begins[block], key_at <= rows_at[block]))
                for j in range(0, PER_GROUP, PAIR):
                    parts = [
                        qbuf[k, :, at * CHUNK + i * D_HEAD:at * CHUNK + (i + 1) * D_HEAD]
                        for i in range(j, j + PAIR)
                    ]
                    logits = lax.dot_general(
                        jnp.concatenate(parts, axis=0), key_tile, (((1,), (1,)), ((), ())),
                        preferred_element_type=jnp.float32,
                    )
                    for i in range(PAIR):
                        rows = pl.ds(k * STACKED + (j + i) * BLOCK, BLOCK)
                        part = logits[i * BLOCK:(i + 1) * BLOCK]
                        low = jnp.where(masks[0], part[:, :D_HEAD], MASKED)
                        high = jnp.where(masks[1], part[:, D_HEAD:], MASKED)
                        sbuf[p, rows, :D_HEAD] = low
                        sbuf[p, rows, D_HEAD:] = high
                        mbuf[rows, :] = jnp.maximum(mbuf[rows, :], jnp.maximum(low, high))
            return 0

        lax.fori_loop(lowest, PIECES, score_tile, 0)
        for i in range(RECV * PER_GROUP):
            rows = pl.ds(i * BLOCK, BLOCK)
            peak = jnp.max(mbuf[rows, :], axis=-1, keepdims=True)
            mbuf[rows, :] = jnp.broadcast_to(peak, (BLOCK, D_HEAD))
        lbuf[...] = jnp.zeros_like(lbuf)
        abuf[...] = jnp.zeros_like(abuf)

        def weigh_tile(p, _):
            value_tile = vbuf[p]
            for i in range(0, RECV * PER_GROUP, PAIR):
                rows = pl.ds(i * BLOCK, PAIR * BLOCK)
                peak = mbuf[rows, :]
                low = jnp.exp2((sbuf[p, rows, :D_HEAD] - peak) * EXP2_SCALE)
                high = jnp.exp2((sbuf[p, rows, D_HEAD:] - peak) * EXP2_SCALE)
                lbuf[rows, :] += low + high
                soft = jnp.concatenate([low.astype(jnp.bfloat16), high.astype(jnp.bfloat16)], axis=1)
                abuf[rows, :] += jnp.dot(soft, value_tile, preferred_element_type=jnp.float32)
            return 0

        lax.fori_loop(lowest, PIECES, weigh_tile, 0)
        for k in range(RECV):
            scored = score[k * BLOCK:(k + 1) * BLOCK, :]
            for j in range(PER_GROUP):
                rows = pl.ds(k * STACKED + j * BLOCK, BLOCK)
                totals = jnp.sum(lbuf[rows, :], axis=-1, keepdims=True)
                into = slice(at * CHUNK + j * D_HEAD, at * CHUNK + (j + 1) * D_HEAD)
                head_out = (abuf[rows, :] / totals).astype(jnp.bfloat16)
                obuf[k, :, into] = head_out
                direction = reward_dir[:, head * CHUNK + j * D_HEAD:head * CHUNK + (j + 1) * D_HEAD]
                scored += head_out.astype(jnp.float32) * direction
            score[k * BLOCK:(k + 1) * BLOCK, :] = scored
            store = pltpu.make_async_copy(
                obuf.at[k, :, pl.ds(at * CHUNK, CHUNK)],
                out.at[pl.ds(k * BLOCK, BLOCK), pl.ds(head * CHUNK, CHUNK)],
                o_sems.at[at, k],
            )
            store.start()
            stores.append(store)
    if earlier:
        score[...] += sum(part[...] for part in earlier)
    if rewards is not None:
        def settle(r, _):
            following = info[jnp.minimum(r + 1, responses - 1)]
            at = jnp.where(r + 1 < responses, following, ranks * ROWS) - 1 - first
            here = jnp.logical_and(at >= 0, at < ROWS)
            row = score[pl.ds(jnp.clip(at, 0, ROWS - 1), 1), :]
            rewards[pl.ds(r, 1), :] = jnp.where(here, row, 0.0)
            return 0

        lax.fori_loop(0, responses, settle, 0)
    for store in stores:
        store.wait()


def attend(
    heads, info, place, q_own, q_outer, q_inner, window, reward_dir, previous, scores, last,
    capacity, responses, ranks,
):
    operands = [info, place, q_own, q_outer, q_inner, *window, reward_dir]
    used = len(operands)
    in_specs = [SMEM, SMEM] + [VMEM] * 10
    aliases = {}
    if previous is not None:
        aliases = {used: 0}
        operands += [previous] + scores
        in_specs += [HBM] + [VMEM] * len(scores)
    taken = len(operands)
    out_shape = [
        jax.ShapeDtypeStruct((ROWS, WIDTH), jnp.bfloat16),
        jax.ShapeDtypeStruct((ROWS, D_HEAD), jnp.float32),
    ]
    if last:
        out_shape.append(jax.ShapeDtypeStruct((responses, D_HEAD), jnp.float32))
    made = taken + len(out_shape)

    def body(*refs):
        attend_kernel(
            responses, ranks, capacity, heads, refs[used + 1:taken], refs[made - 1] if last else None,
            *refs[:used], *refs[taken:taken + 2], *refs[made:],
        )

    number = len(heads)
    return pl.pallas_call(
        body,
        out_shape=out_shape,
        in_specs=in_specs,
        out_specs=[HBM] + [VMEM] * (len(out_shape) - 1),
        scratch_shapes=[
            pltpu.VMEM((PIECES, ROWS, D_HEAD), jnp.bfloat16),
            pltpu.VMEM((PIECES, ROWS, D_HEAD), jnp.bfloat16),
            pltpu.VMEM((RECV, BLOCK, number * CHUNK), jnp.bfloat16),
            pltpu.VMEM((RECV, BLOCK, number * CHUNK), jnp.bfloat16),
            pltpu.VMEM((PIECES, RECV * STACKED, ROWS), jnp.float32),
            pltpu.VMEM((RECV * STACKED, D_HEAD), jnp.float32),
            pltpu.VMEM((RECV * STACKED, D_HEAD), jnp.float32),
            pltpu.VMEM((RECV * STACKED, D_HEAD), jnp.float32),
            pltpu.SemaphoreType.DMA((number, RECV)),
        ],
        input_output_aliases=aliases,
        compiler_params=SLIM,
        cost_estimate=pl.CostEstimate(
            flops=4 * number * RECV * STACKED * PIECES * ROWS * D_HEAD,
            bytes_accessed=2 * number * 1024 * 1024,
            transcendentals=number * RECV * STACKED * PIECES * ROWS,
        ),
    )(*operands)


def shards(queries, keys, values, block_counts, segment_ids, reward_dir):
    ranks = lax.axis_size("dp")
    rank = lax.axis_index("dp")
    capacity = queries.shape[0] // BLOCK
    responses = ranks * 2 // REACH
    place = rank.astype(jnp.int32).reshape(1)

    kv_outer, kv_inner, q_first = first_stage(block_counts, place, queries, keys, values)
    kv_outer = outer_pairs(kv_outer, ranks)
    kv_inner = inner_pairs(kv_inner, ranks)
    q_outer = [outer_pairs(q_first, ranks)]

    ids = jnp.arange(responses, dtype=jnp.int32)
    smaller = jnp.sum((segment_ids[None, :] < ids[:, None]).astype(jnp.int32), axis=1)
    marks = jnp.where(jnp.arange(ranks, dtype=jnp.int32) == rank, block_counts[0], 0)
    info = lax.psum(jnp.concatenate([smaller, marks]), "dp")

    own, q_own = pack(info, place, queries, keys, values, kv_outer, kv_inner, responses, ranks)
    two = shifted(own, "dp", 2)
    four = shifted(own, "dp", 4)
    pairs = range(ranks // 2)
    sib_own = lax.ppermute(own, "dp", [(2 * m, 2 * m + 1) for m in pairs])

    *q_later, q_inner = second_stage(block_counts, place, queries)
    for part in q_later:
        q_outer.append(outer_pairs(part, ranks))
    q_inner = inner_pairs(q_inner, ranks)

    sib_two = inner_pairs(two, ranks)
    sib_four = lax.ppermute(four, "dp", [(2 * m + 1, 2 * m) for m in pairs])
    window = (own, two, four, sib_own, sib_two, sib_four)

    direction = reward_dir.reshape(1, -1)
    attn_out, scores = None, []
    for i, heads in enumerate(SPLIT):
        last = i == len(SPLIT) - 1
        attn_out, score, *settled = attend(
            heads, info, place, q_own, q_outer[i], q_inner, window, direction, attn_out, scores,
            last, capacity, responses, ranks,
        )
        scores = [score]
    rewards = lax.psum(jnp.sum(settled[0], axis=1), "dp")
    return (attn_out, rewards)


def solution(mesh):
    return jax.shard_map(
        shards,
        mesh=mesh,
        in_specs=(
            P(("groups", "dp"), None),
            P(("groups", "dp"), None),
            P(("groups", "dp"), None),
            P(("groups", "dp")),
            P(("groups", "dp")),
            P(),
        ),
        out_specs=(P(("groups", "dp"), None), P("groups")),
        check_vma=False,
    )
```

time: 310 us -> 139 us (0.45)
  starting transfers between devices: 123 us -> 16.3 us
  matrix products: 43.2 us -> 0 us
  local copies, waits for them, and re-layouts: 34.3 us -> 3.42 us
  other arithmetic: 29.4 us -> 0.31 us
  Pallas kernels: 0 us -> 24.2 us
  waiting for transfers between devices: 0.04 us -> 17.9 us
    ppermute x15 -> x2, starting transfers between devices: 123 us -> 2.64 us  [shifted(): return lax.ppermute(block, axis, route)]
    dot_general x9 -> x0, matrix products: 43.2 us -> none  [the longest x4 23.6 us: attend(): jnp.dot(soft_weights, value_heads[:, head_index], preferred_element_type=...]
    pallas_call x0 -> x6, Pallas kernels: none -> 24.2 us  [the longest x3 13.2 us: attend(): pl.pallas_call(body, out_shape=out_shape, in_specs=in_specs, out_specs=[H...]
    gather x9 -> x0, local copies, waits for them, and re-layouts: 17.2 us -> none  [outgoing(): chosen = jnp.take(blocks, bounded, axis=0)]
    ppermute x15 -> x2, waiting for transfers between devices: 0.04 us -> 16.7 us  [shifted(): return lax.ppermute(block, axis, route)]
    unnamed x1 -> x0, blocking collectives: 15.8 us -> none
    reduce_sum x5 -> x2, other arithmetic: 15.2 us -> 0.23 us  [the longest x1 0.12 us: shards(): rewards = lax.psum(jnp.sum(settled[0], axis=1), 'dp')]
    psum x1 -> x2, blocking collectives: 59.4 us -> 73.5 us  [the longest x1 41.8 us: shards(): rewards = lax.psum(jnp.sum(settled[0], axis=1), 'dp')]
  transfers between devices with their start and end apart: 15 -> 11, of which waited for: 0 -> 2; matrix products, arithmetic and copies ran while one was open for 11% -> 0% of each run, Pallas kernels for 0% -> 12%
where the time goes in v1:
time: 139 us; the launch traced here: 137 us
  blocking collectives  73.5 us (53%)
  Pallas kernels  24.2 us (17%)
  waiting for transfers between devices  17.9 us (13%)
  starting transfers between devices  16.3 us (12%)
  local copies, waits for them, and re-layouts  3.42 us (2%)
  between operations  1.5 us (1%)
    psum x1, blocking collectives, shards(): rewards = lax.psum(jnp.sum(settled[0], axis=1), 'dp')  41.8 us
    psum x1, blocking collectives, shards(): info = lax.psum(jnp.concatenate([smaller, marks]), 'dp')  31.7 us
    ppermute x2, waiting for transfers between devices, shifted(): return lax.ppermute(block, axis, route)  16.7 us
    pallas_call x3, Pallas kernels, attend(): pl.pallas_call(body, out_shape=out_shape, in_specs=in_specs, out_specs=[H...  13.2 us
    ppermute x1, starting transfers between devices, shards(): sib_own = lax.ppermute(own, 'dp', [(2 * m, 2 * m + 1) for m in pairs])  5.07 us
    pallas_call x1, Pallas kernels, pack(): pl.pallas_call(functools.partial(pack_kernel, responses, ranks, capacity)...  4.63 us
    ppermute x3, starting transfers between devices, inner_pairs(): return lax.ppermute(block, 'dp', [(i, i ^ 1) for i in range(ranks)])  4.54 us
    pallas_call x1, Pallas kernels, second_stage(): pl.pallas_call(functools.partial(second_stage_kernel, capacity), out_shap...  3.91 us
  transfers between devices with their start and end apart: 11, of which 2 were waited for; matrix products, arithmetic and copies ran while one was open for 0% of the time, Pallas kernels for 12%

profile of v1, /device:TPU:0, one launch (start us, length us, event | category | flops | bytes accessed | tf_op | source)
XLA Modules:
  0.0 137.2 jit_solution(16062378013777306312)
XLA Ops:
  1.3 3.9 %second_stage.1 = (bf16[256,2048]{1,0:T(8,128)(2,1)}, bf16[256,1024]{1,0:T(8,128)(2,1)}, bf16[256,4096]{1,0:T(8,128)(2,1)}) custom-call(s32[1]{0:T(128)} %copy.12.counts, s32[1]{0:T(128)} %bitcast.1.place.refs_1_, bf16[768,4096]{1,0:T(8,128)(2,1)} %queries.5), custom_call_target="tpu_custom_call" | custom-call | tf_op jit(solution)/shard_map/second_stage/pallas_call | solution.py:117
  5.2 0.0 copy-start.7
  5.2 0.6 collective-permute-start.3
  5.8 2.5 %first_stage.1 = (bf16[256,1024]{1,0:T(8,128)(2,1)}, bf16[256,1024]{1,0:T(8,128)(2,1)}, bf16[256,1024]{1,0:T(8,128)(2,1)}) custom-call(s32[1]{0:T(128)} %copy.12.counts, s32[1]{0:T(128)} %bitcast.1.place.refs_1_, bf16[768,4096]{1,0:T(8,128)(2,1)} %queries.5, bf16[768,512]{1,0:T(8,128)(2,1)} %keys.3, bf16[768,512]{1,0:T(8,128)(2,1)} %values.3), custom_call_target="tpu_custom_call" | custom-call | tf_op jit(solution)/shard_map/first_stage/pallas_call | solution.py:92
  8.3 0.7 collective-permute-start
  9.0 4.0 %collective-permute-start.1 = (bf16[256,1024]{1,0:T(8,128)(2,1)}, bf16[256,1024]{1,0:T(8,128)(2,1)}, u32[]{:S(2)}, u32[]{:S(2)}) collective-permute-start(bf16[256,1024]{1,0:T(8,128)(2,1)} %get-tuple-element.17), channel_id=1, source_target_pairs={{0,1},{1,0},{2,3},{3,2},{4,5},{5,4},{6,7},{7,6},{8,9},{9,8},{10,11... | collective-permute-start | bytes 1572872 | tf_op jit(solution)/shard_map/ppermute | solution.py:43
  13.0 0.7 collective-permute-start.10
  13.7 0.1 convert_reduce_fusion
  13.8 0.1 pad_add_fusion
  13.9 31.7 %psum.14.info.refs_0_ = s32[24]{0:T(128)} all-reduce(s32[24]{0:T(128)S(1)} %pad_add_fusion), channel_id=1, replica_groups=mesh['groups'=2,'dp'=16] {'dp'}, use_global_device_ids=true, to_apply=%region_1.2 | all-reduce | flops 24 | bytes 192 | tf_op jit(solution)/shard_map/psum | solution.py:422
  45.6 0.0 collective-permute-done.outer
  45.6 0.8 copy-done.4
  46.4 4.6 %pack.1 = (bf16[256,1024]{1,0:T(8,128)(2,1)}, bf16[256,4096]{1,0:T(8,128)(2,1)}) custom-call(s32[24]{0:T(128)} %psum.14.info.refs_0_, s32[1]{0:T(128)} %bitcast.1.place.refs_1_, bf16[768,4096]{1,0:T(8,128)(2,1)} %queries.5, bf16[768,512]{1,0:T(8,128)(2,1)} %keys.3, bf16[768,512]{1,0:T(8,128)(2,1)} %values.3, bf16[256,1024]{1,0:T(8,128)(2,1)} %copy-done.4, ...), custom_call_target="tpu_custom_call" | custom-call | tf_op jit(solution)/shard_map/pack/pallas_call | solution.py:182
  51.0 1.3 collective-permute-start.5
  52.3 1.3 collective-permute-start.4
  53.7 0.7 collective-permute-start.9
  54.4 0.0 collective-permute-done.10.refs_3_
  54.4 5.1 %collective-permute-start.6 = (bf16[256,1024]{1,0:T(8,128)(2,1)}, bf16[256,1024]{1,0:T(8,128)(2,1)S(1)}, u32[]{:S(2)}, u32[]{:S(2)}) collective-permute-start(bf16[256,1024]{1,0:T(8,128)(2,1)} %get-tuple-element.21.refs_5_), channel_id=1, source_target_pairs={{0,1},{2,3},{4,5},{6,7},{8,9},{10,11},{12,13},{14,15},{16,17},{18,... | collective-permute-start | bytes 1572872 | tf_op jit(solution)/shard_map/ppermute | solution.py:428
  59.5 0.0 collective-permute-done.5.refs_7_
  59.5 1.3 collective-permute-start.8
  60.8 16.7 %collective-permute-done.4.refs_6_ = bf16[256,1024]{1,0:T(8,128)(2,1)S(1)} collective-permute-done((bf16[256,1024]{1,0:T(8,128)(2,1)}, bf16[256,1024]{1,0:T(8,128)(2,1)S(1)}, u32[]{:S(2)}, u32[]{:S(2)}) %collective-permute-start.4) | collective-permute-done | bytes 524320 | tf_op jit(solution)/shard_map/ppermute | solution.py:39
  77.5 0.0 collective-permute-start.7
  77.5 0.7 collective-permute-start.2
  78.2 1.2 collective-permute-done.7.refs_9_
  79.4 0.0 copy-start
  79.4 1.6 %copy-done = bf16[256,4096]{1,0:T(8,128)(2,1)S(1)} copy-done((bf16[256,4096]{1,0:T(8,128)(2,1)S(1)}, bf16[256,4096]{1,0:T(8,128)(2,1)}, u32[]{:S(2)}) %copy-start) | copy-done | bytes 2097176
  81.0 1.0 copy-done.1
  82.0 3.5 %shard_map.77 = (bf16[256,4096]{1,0:T(8,128)(2,1)}, f32[256,128]{1,0:T(8,128)S(1)}) custom-call(s32[24]{0:T(128)S(1)} %copy-done.3, s32[1]{0:T(128)} %bitcast.1.place.refs_1_, bf16[256,4096]{1,0:T(8,128)(2,1)S(1)} %copy-done, bf16[256,1024]{1,0:T(8,128)(2,1)S(1)} %collective-permute-done.10.refs_3_, bf16[256,4096]{1,0:T(8,128)(2,1)S(1)} %collective-permute-done.3.refs_4_, ...), custom_call_target="tpu_custom_call" | custom-call | flops 1342177280 | bytes 2097152 | tf_op jit(solution)/shard_map/pallas_call | solution.py:381
  85.6 5.4 %shard_map.78 = (bf16[256,4096]{1,0:T(8,128)(2,1)}, f32[256,128]{1,0:T(8,128)S(1)}) custom-call(s32[24]{0:T(128)S(1)} %copy-done.3, s32[1]{0:T(128)} %bitcast.1.place.refs_1_, bf16[256,4096]{1,0:T(8,128)(2,1)S(1)} %copy-done, bf16[256,2048]{1,0:T(8,128)(2,1)S(1)} %collective-permute-done.9.refs_3_, ...), custom_call_target="tpu_custom_call", output_to_operand_aliasing={{0}: (12, {})} | custom-call | flops 2684354560 | bytes 4194304 | tf_op jit(solution)/shard_map/pallas_call | solution.py:381
  91.0 4.2 %shard_map.79 = (bf16[256,4096]{1,0:T(8,128)(2,1)}, f32[256,128]{1,0:T(8,128)}, f32[8,128]{1,0:T(8,128)S(1)}) custom-call(s32[24]{0:T(128)S(1)} %copy-done.3, s32[1]{0:T(128)} %bitcast.1.place.refs_1_, bf16[256,4096]{1,0:T(8,128)(2,1)S(1)} %copy-done, bf16[256,1024]{1,0:T(8,128)(2,1)S(1)} %collective-permute-done.2.refs_3_, ...), custom_call_target="tpu_custom_call", output_to_operand_aliasing={{0}: (12, {})} | custom-call | flops 1342177280 | bytes 2097152 | tf_op jit(solution)/shard_map/pallas_call | solution.py:381
  95.2 0.1 reduce_sum.19
  95.4 41.8 %psum.15 = f32[8]{0:T(128)} all-reduce(f32[8]{0:T(128)S(1)} %reduce_sum.19), channel_id=1, replica_groups=mesh['groups'=2,'dp'=16] {'dp'}, use_global_device_ids=true, to_apply=%region_3.4 | all-reduce | flops 8 | bytes 64 | tf_op jit(solution)/shard_map/psum | solution.py:448
  (18 shorter events, 0.0 us)
Async XLA Ops:
  5.2 8.5 %copy-start.7 = (s32[256]{0:T(256)S(1)}, s32[256]{0:T(256)}, u32[]{:S(2)}) copy-start(s32[256]{0:T(256)} %param.10) | copy-start | bytes 3076
  5.2 74.2 %collective-permute-start.3 = (bf16[256,4096]{1,0:T(8,128)(2,1)}, bf16[256,4096]{1,0:T(8,128)(2,1)S(1)}, u32[]{:S(2)}, u32[]{:S(2)}) collective-permute-start(bf16[256,4096]{1,0:T(8,128)(2,1)} %get-tuple-element.20), channel_id=1, source_target_pairs={{0,1},{1,0},{2,3},{3,2},{4,5},{5,4},{6,7},{7,6},{8,9},{9,8},{10,11... | collective-permute-start | bytes 6291464 | tf_op jit(solution)/shard_map/ppermute | solution.py:43
  8.3 37.2 %collective-permute-start = (bf16[256,1024]{1,0:T(8,128)(2,1)}, bf16[256,1024]{1,0:T(8,128)(2,1)S(1)}, u32[]{:S(2)}, u32[]{:S(2)}) collective-permute-start(bf16[256,1024]{1,0:T(8,128)(2,1)} %get-tuple-element.16), channel_id=1, source_target_pairs={{1,2},{2,1},{3,4},{4,3},{5,6},{6,5},{7,8},{8,7},{9,10},{10,9},{11,... | collective-permute-start | bytes 1572872 | tf_op jit(solution)/shard_map/ppermute | solution.py:50
  9.0 36.6 %collective-permute-start.1 = (bf16[256,1024]{1,0:T(8,128)(2,1)}, bf16[256,1024]{1,0:T(8,128)(2,1)}, u32[]{:S(2)}, u32[]{:S(2)}) collective-permute-start(bf16[256,1024]{1,0:T(8,128)(2,1)} %get-tuple-element.17), channel_id=1, source_target_pairs={{0,1},{1,0},{2,3},{3,2},{4,5},{5,4},{6,7},{7,6},{8,9},{9,8},{10,11... | collective-permute-start | bytes 1572872 | tf_op jit(solution)/shard_map/ppermute | solution.py:43
  13.0 41.4 %collective-permute-start.10 = (bf16[256,1024]{1,0:T(8,128)(2,1)}, bf16[256,1024]{1,0:T(8,128)(2,1)S(1)}, u32[]{:S(2)}, u32[]{:S(2)}) collective-permute-start(bf16[256,1024]{1,0:T(8,128)(2,1)} %get-tuple-element.23), channel_id=1, source_target_pairs={{1,2},{2,1},{3,4},{4,3},{5,6},{6,5},{7,8},{8,7},{9,10},{10,9},{11,... | collective-permute-start | bytes 1572872 | tf_op jit(solution)/shard_map/ppermute | solution.py:50
  45.5 8.1 %copy-start.5 = (bf16[256,2048]{1,0:T(8,128)(2,1)S(1)}, bf16[256,2048]{1,0:T(8,128)(2,1)}, u32[]{:S(2)}) copy-start(bf16[256,2048]{1,0:T(8,128)(2,1)} %get-tuple-element.22) | copy-start | bytes 3145732
  45.5 31.9 %copy-start.6 = (bf16[256,1024]{1,0:T(8,128)(2,1)S(1)}, bf16[256,1024]{1,0:T(8,128)(2,1)}, u32[]{:S(2)}) copy-start(bf16[256,1024]{1,0:T(8,128)(2,1)} %get-tuple-element.19) | copy-start | bytes 1572868
  45.5 33.8 %copy-start.2 = (f32[4096]{0:T(1024)S(1)}, f32[4096]{0:T(1024)}, u32[]{:S(2)}) copy-start(f32[4096]{0:T(1024)} %param.11) | copy-start | bytes 49156
  45.5 33.8 %copy-start.3 = (s32[24]{0:T(128)S(1)}, s32[24]{0:T(128)}, u32[]{:S(2)}) copy-start(s32[24]{0:T(128)} %psum.14.info.refs_0_) | copy-start | bytes 292
  45.6 0.8 copy-start.4
  51.0 8.5 %collective-permute-start.5 = (bf16[256,1024]{1,0:T(8,128)(2,1)}, bf16[256,1024]{1,0:T(8,128)(2,1)S(1)}, u32[]{:S(2)}, u32[]{:S(2)}) collective-permute-start(bf16[256,1024]{1,0:T(8,128)(2,1)} %get-tuple-element.21.refs_5_), channel_id=1, source_target_pairs={{0,4},{1,5},{2,6},{3,7},{4,8},{5,9},{6,10},{7,11},{8,12},{9,13},{1... | collective-permute-start | bytes 1572872 | tf_op jit(solution)/shard_map/ppermute | solution.py:39
  52.3 25.1 %collective-permute-start.4 = (bf16[256,1024]{1,0:T(8,128)(2,1)}, bf16[256,1024]{1,0:T(8,128)(2,1)S(1)}, u32[]{:S(2)}, u32[]{:S(2)}) collective-permute-start(bf16[256,1024]{1,0:T(8,128)(2,1)} %get-tuple-element.21.refs_5_), channel_id=1, source_target_pairs={{0,2},{1,3},{2,4},{3,5},{4,6},{5,7},{6,8},{7,9},{8,10},{9,11},{10,... | collective-permute-start | bytes 1572872 | tf_op jit(solution)/shard_map/ppermute | solution.py:39
  53.7 31.9 %collective-permute-start.9 = (bf16[256,2048]{1,0:T(8,128)(2,1)S(1)}, bf16[256,2048]{1,0:T(8,128)(2,1)S(1)}, u32[]{:S(2)}, u32[]{:S(2)}) collective-permute-start(bf16[256,2048]{1,0:T(8,128)(2,1)S(1)} %copy-done.5), channel_id=1, source_target_pairs={{1,2},{2,1},{3,4},{4,3},{5,6},{6,5},{7,8},{8,7},{9,10},{10,9},{11,... | collective-permute-start | bytes 3145736 | tf_op jit(solution)/shard_map/ppermute | solution.py:50
  54.4 23.1 %collective-permute-start.6 = (bf16[256,1024]{1,0:T(8,128)(2,1)}, bf16[256,1024]{1,0:T(8,128)(2,1)S(1)}, u32[]{:S(2)}, u32[]{:S(2)}) collective-permute-start(bf16[256,1024]{1,0:T(8,128)(2,1)} %get-tuple-element.21.refs_5_), channel_id=1, source_target_pairs={{0,1},{2,3},{4,5},{6,7},{8,9},{10,11},{12,13},{14,15},{16,17},{18,... | collective-permute-start | bytes 1572872 | tf_op jit(solution)/shard_map/ppermute | solution.py:428
  59.5 18.7 %collective-permute-start.8 = (bf16[256,1024]{1,0:T(8,128)(2,1)S(1)}, bf16[256,1024]{1,0:T(8,128)(2,1)S(1)}, u32[]{:S(2)}, u32[]{:S(2)}) collective-permute-start(bf16[256,1024]{1,0:T(8,128)(2,1)S(1)} %collective-permute-done.5.refs_7_), channel_id=1, source_target_pairs={{1,0},{3,2},{5,4},{7,6},{9,8},{11,10},{13,12},{15,14},{17,16},{19,... | collective-permute-start | bytes 1572872 | tf_op jit(solution)/shard_map/ppermute | solution.py:436
  77.5 1.9 %collective-permute-start.7 = (bf16[256,1024]{1,0:T(8,128)(2,1)S(1)}, bf16[256,1024]{1,0:T(8,128)(2,1)S(1)}, u32[]{:S(2)}, u32[]{:S(2)}) collective-permute-start(bf16[256,1024]{1,0:T(8,128)(2,1)S(1)} %collective-permute-done.4.refs_6_), channel_id=1, source_target_pairs={{0,1},{1,0},{2,3},{3,2},{4,5},{5,4},{6,7},{7,6},{8,9},{9,8},{10,11... | collective-permute-start | bytes 1572872 | tf_op jit(solution)/shard_map/ppermute | solution.py:43
  77.5 13.5 %collective-permute-start.2 = (bf16[256,1024]{1,0:T(8,128)(2,1)S(1)}, bf16[256,1024]{1,0:T(8,128)(2,1)S(1)}, u32[]{:S(2)}, u32[]{:S(2)}) collective-permute-start(bf16[256,1024]{1,0:T(8,128)(2,1)S(1)} %copy-done.6), channel_id=1, source_target_pairs={{1,2},{2,1},{3,4},{4,3},{5,6},{6,5},{7,8},{8,7},{9,10},{10,9},{11,... | collective-permute-start | bytes 1572872 | tf_op jit(solution)/shard_map/ppermute | solution.py:50
  79.4 1.6 %copy-start = (bf16[256,4096]{1,0:T(8,128)(2,1)S(1)}, bf16[256,4096]{1,0:T(8,128)(2,1)}, u32[]{:S(2)}) copy-start(bf16[256,4096]{1,0:T(8,128)(2,1)} %get-tuple-element.18.refs_2_) | copy-start | bytes 6291460
  81.0 1.0 copy-start.1

commit v2 on v1

--- a/solution.py
+++ b/solution.py
@@ -48,6 +48,16 @@
     for low in range(1, ranks - 1, 2):
         route += [(low, low + 1), (low + 1, low)]
     return lax.ppermute(block, "dp", route)
+
+
+def total_over(part, ranks):
+    if ranks & (ranks - 1):
+        return lax.psum(part, "dp")
+    bit = 1
+    while bit < ranks:
+        part = part + lax.ppermute(part, "dp", [(i, i ^ bit) for i in range(ranks)])
+        bit *= 2
+    return part
 
 
 def block_rows(index):
@@ -445,7 +455,7 @@
             last, capacity, responses, ranks,
         )
         scores = [score]
-    rewards = lax.psum(jnp.sum(settled[0], axis=1), "dp")
+    rewards = total_over(jnp.sum(settled[0], axis=1), ranks)
     return (attn_out, rewards)
 
 

time: 139 us -> 128 us (0.921); the launches traced: 137 us -> 128 us
  blocking collectives: 73.5 us -> 31.7 us
  starting transfers between devices: 16.3 us -> 43 us
  waiting for transfers between devices: 17.9 us -> 23.3 us
    psum x1 -> x0, blocking collectives: 41.8 us -> none  [shards(): rewards = lax.psum(jnp.sum(settled[0], axis=1), 'dp')]
    ppermute x0 -> x4, starting transfers between devices: none -> 26.6 us  [total_over(): part = part + lax.ppermute(part, 'dp', [(i, i ^ bit) for i in range(ranks)])]
    ppermute x0 -> x4, waiting for transfers between devices: none -> 5.46 us  [total_over(): part = part + lax.ppermute(part, 'dp', [(i, i ^ bit) for i in range(ranks)])]
  transfers between devices with their start and end apart: 11 -> 15, of which waited for: 2 -> 6; matrix products, arithmetic and copies ran while one was open for 0% -> 0% of each run, Pallas kernels for 12% -> 13%
where the time goes in v2:
time: 128 us
  starting transfers between devices  43 us (34%)
  blocking collectives  31.7 us (25%)
  Pallas kernels  24.3 us (19%)
  waiting for transfers between devices  23.3 us (18%)
  local copies, waits for them, and re-layouts  3.43 us (3%)
  between operations  1.5 us (1%)
    psum x1, blocking collectives, shards(): info = lax.psum(jnp.concatenate([smaller, marks]), 'dp')  31.7 us
    ppermute x4, starting transfers between devices, total_over(): part = part + lax.ppermute(part, 'dp', [(i, i ^ bit) for i in range(ranks)])  26.6 us
    ppermute x2, waiting for transfers between devices, shifted(): return lax.ppermute(block, axis, route)  16.7 us
    pallas_call x3, Pallas kernels, attend(): pl.pallas_call(body, out_shape=out_shape, in_specs=in_specs, out_specs=[H...  13.2 us
    ppermute x4, waiting for transfers between devices, total_over(): part = part + lax.ppermute(part, 'dp', [(i, i ^ bit) for i in range(ranks)])  5.46 us
    ppermute x1, starting transfers between devices, shards(): sib_own = lax.ppermute(own, 'dp', [(2 * m, 2 * m + 1) for m in pairs])  5.07 us
    pallas_call x1, Pallas kernels, pack(): pl.pallas_call(functools.partial(pack_kernel, responses, ranks, capacity)...  4.63 us
    ppermute x3, starting transfers between devices, inner_pairs(): return lax.ppermute(block, 'dp', [(i, i ^ 1) for i in range(ranks)])  4.54 us
  transfers between devices with their start and end apart: 15, of which 6 were waited for; matrix products, arithmetic and copies ran while one was open for 0% of the time, Pallas kernels for 13%

profile of v2, /device:TPU:0, one launch (start us, length us, event | category | flops | bytes accessed | tf_op | source)
XLA Modules:
  0.0 128.0 jit_solution(13108318519415314916)
XLA Ops:
  1.3 3.9 %second_stage.1 = (bf16[256,2048]{1,0:T(8,128)(2,1)}, bf16[256,1024]{1,0:T(8,128)(2,1)}, bf16[256,4096]{1,0:T(8,128)(2,1)}) custom-call(s32[1]{0:T(128)} %copy.12.counts, s32[1]{0:T(128)} %bitcast.1.place.refs_1_, bf16[768,4096]{1,0:T(8,128)(2,1)} %queries.5), custom_call_target="tpu_custom_call" | custom-call | tf_op jit(solution)/shard_map/second_stage/pallas_call | solution.py:127
  5.2 0.6 collective-permute-start.3
  5.8 2.5 %first_stage.1 = (bf16[256,1024]{1,0:T(8,128)(2,1)}, bf16[256,1024]{1,0:T(8,128)(2,1)}, bf16[256,1024]{1,0:T(8,128)(2,1)}) custom-call(s32[1]{0:T(128)} %copy.12.counts, s32[1]{0:T(128)} %bitcast.1.place.refs_1_, bf16[768,4096]{1,0:T(8,128)(2,1)} %queries.5, bf16[768,512]{1,0:T(8,128)(2,1)} %keys.3, bf16[768,512]{1,0:T(8,128)(2,1)} %values.3), custom_call_target="tpu_custom_call" | custom-call | tf_op jit(solution)/shard_map/first_stage/pallas_call | solution.py:102
  8.3 0.7 collective-permute-start
  9.0 4.0 %collective-permute-start.1 = (bf16[256,1024]{1,0:T(8,128)(2,1)}, bf16[256,1024]{1,0:T(8,128)(2,1)}, u32[]{:S(2)}, u32[]{:S(2)}) collective-permute-start(bf16[256,1024]{1,0:T(8,128)(2,1)} %get-tuple-element.17), channel_id=1, source_target_pairs={{0,1},{1,0},{2,3},{3,2},{4,5},{5,4},{6,7},{7,6},{8,9},{9,8},{10,11... | collective-permute-start | bytes 1572872 | tf_op jit(solution)/shard_map/ppermute | solution.py:43
  13.0 0.7 collective-permute-start.10
  13.9 31.7 %psum.7.info.refs_0_ = s32[24]{0:T(128)} all-reduce(s32[24]{0:T(128)S(1)} %pad_add_fusion), channel_id=1, replica_groups=mesh['groups'=2,'dp'=16] {'dp'}, use_global_device_ids=true, to_apply=%region_1.2 | all-reduce | flops 24 | bytes 192 | tf_op jit(solution)/shard_map/psum | solution.py:432
  45.6 0.8 copy-done.4
  46.4 4.6 %pack.1 = (bf16[256,1024]{1,0:T(8,128)(2,1)}, bf16[256,4096]{1,0:T(8,128)(2,1)}) custom-call(s32[24]{0:T(128)} %psum.7.info.refs_0_, s32[1]{0:T(128)} %bitcast.1.place.refs_1_, bf16[768,4096]{1,0:T(8,128)(2,1)} %queries.5, bf16[768,512]{1,0:T(8,128)(2,1)} %keys.3, bf16[768,512]{1,0:T(8,128)(2,1)} %values.3, bf16[256,1024]{1,0:T(8,128)(2,1)} %copy-done.4, ...), custom_call_target="tpu_custom_call" | custom-call | tf_op jit(solution)/shard_map/pack/pallas_call | solution.py:192
  51.0 1.3 %collective-permute-start.5 = (bf16[256,1024]{1,0:T(8,128)(2,1)}, bf16[256,1024]{1,0:T(8,128)(2,1)S(1)}, u32[]{:S(2)}, u32[]{:S(2)}) collective-permute-start(bf16[256,1024]{1,0:T(8,128)(2,1)} %get-tuple-element.21.refs_5_), channel_id=1, source_target_pairs={{0,4},{1,5},{2,6},{3,7},{4,8},{5,9},{6,10},{7,11},{8,12},{9,13},{1... | collective-permute-start | bytes 1572872 | tf_op jit(solution)/shard_map/ppermute | solution.py:39
  52.4 1.3 %collective-permute-start.4 = (bf16[256,1024]{1,0:T(8,128)(2,1)}, bf16[256,1024]{1,0:T(8,128)(2,1)S(1)}, u32[]{:S(2)}, u32[]{:S(2)}) collective-permute-start(bf16[256,1024]{1,0:T(8,128)(2,1)} %get-tuple-element.21.refs_5_), channel_id=1, source_target_pairs={{0,2},{1,3},{2,4},{3,5},{4,6},{5,7},{6,8},{7,9},{8,10},{9,11},{10,... | collective-permute-start | bytes 1572872 | tf_op jit(solution)/shard_map/ppermute | solution.py:39
  53.7 0.7 collective-permute-start.9
  54.5 5.1 %collective-permute-start.6 = (bf16[256,1024]{1,0:T(8,128)(2,1)}, bf16[256,1024]{1,0:T(8,128)(2,1)S(1)}, u32[]{:S(2)}, u32[]{:S(2)}) collective-permute-start(bf16[256,1024]{1,0:T(8,128)(2,1)} %get-tuple-element.21.refs_5_), channel_id=1, source_target_pairs={{0,1},{2,3},{4,5},{6,7},{8,9},{10,11},{12,13},{14,15},{16,17},{18,... | collective-permute-start | bytes 1572872 | tf_op jit(solution)/shard_map/ppermute | solution.py:438
  59.5 1.3 %collective-permute-start.8 = (bf16[256,1024]{1,0:T(8,128)(2,1)S(1)}, bf16[256,1024]{1,0:T(8,128)(2,1)S(1)}, u32[]{:S(2)}, u32[]{:S(2)}) collective-permute-start(bf16[256,1024]{1,0:T(8,128)(2,1)S(1)} %collective-permute-done.5.refs_7_), channel_id=1, source_target_pairs={{1,0},{3,2},{5,4},{7,6},{9,8},{11,10},{13,12},{15,14},{17,16},{19,... | collective-permute-start | bytes 1572872 | tf_op jit(solution)/shard_map/ppermute | solution.py:446
  60.8 16.7 %collective-permute-done.4.refs_6_ = bf16[256,1024]{1,0:T(8,128)(2,1)S(1)} collective-permute-done((bf16[256,1024]{1,0:T(8,128)(2,1)}, bf16[256,1024]{1,0:T(8,128)(2,1)S(1)}, u32[]{:S(2)}, u32[]{:S(2)}) %collective-permute-start.4) | collective-permute-done | bytes 524320 | tf_op jit(solution)/shard_map/ppermute | solution.py:39
  77.5 0.7 collective-permute-start.2
  78.2 1.2 collective-permute-done.7.refs_9_
  79.4 1.6 %copy-done = bf16[256,4096]{1,0:T(8,128)(2,1)S(1)} copy-done((bf16[256,4096]{1,0:T(8,128)(2,1)S(1)}, bf16[256,4096]{1,0:T(8,128)(2,1)}, u32[]{:S(2)}) %copy-start) | copy-done | bytes 2097176
  81.0 1.0 copy-done.1
  82.1 3.5 %shard_map.77 = (bf16[256,4096]{1,0:T(8,128)(2,1)}, f32[256,128]{1,0:T(8,128)S(1)}) custom-call(s32[24]{0:T(128)S(1)} %copy-done.3, s32[1]{0:T(128)} %bitcast.1.place.refs_1_, bf16[256,4096]{1,0:T(8,128)(2,1)S(1)} %copy-done, bf16[256,1024]{1,0:T(8,128)(2,1)S(1)} %collective-permute-done.10.refs_3_, bf16[256,4096]{1,0:T(8,128)(2,1)S(1)} %collective-permute-done.3.refs_4_, ...), custom_call_target="tpu_custom_call" | custom-call | flops 1342177280 | bytes 2097152 | tf_op jit(solution)/shard_map/pallas_call | solution.py:391
  85.6 5.4 %shard_map.78 = (bf16[256,4096]{1,0:T(8,128)(2,1)}, f32[256,128]{1,0:T(8,128)S(1)}) custom-call(s32[24]{0:T(128)S(1)} %copy-done.3, s32[1]{0:T(128)} %bitcast.1.place.refs_1_, bf16[256,4096]{1,0:T(8,128)(2,1)S(1)} %copy-done, bf16[256,2048]{1,0:T(8,128)(2,1)S(1)} %collective-permute-done.9.refs_3_, ...), custom_call_target="tpu_custom_call", output_to_operand_aliasing={{0}: (12, {})} | custom-call | flops 2684354560 | bytes 4194304 | tf_op jit(solution)/shard_map/pallas_call | solution.py:391
  91.1 4.2 %shard_map.79 = (bf16[256,4096]{1,0:T(8,128)(2,1)}, f32[256,128]{1,0:T(8,128)}, f32[8,128]{1,0:T(8,128)S(1)}) custom-call(s32[24]{0:T(128)S(1)} %copy-done.3, s32[1]{0:T(128)} %bitcast.1.place.refs_1_, bf16[256,4096]{1,0:T(8,128)(2,1)S(1)} %copy-done, bf16[256,1024]{1,0:T(8,128)(2,1)S(1)} %collective-permute-done.2.refs_3_, ...), custom_call_target="tpu_custom_call", output_to_operand_aliasing={{0}: (12, {})} | custom-call | flops 1342177280 | bytes 2097152 | tf_op jit(solution)/shard_map/pallas_call | solution.py:391
  95.3 0.1 reduce_sum.19
  95.4 9.6 %collective-permute-start.11 = (f32[8]{0:T(128)S(1)}, f32[8]{0:T(128)S(1)}, u32[]{:S(2)}, u32[]{:S(2)}) collective-permute-start(f32[8]{0:T(128)S(1)} %reduce_sum.19), channel_id=1, source_target_pairs={{0,1},{1,0},{2,3},{3,2},{4,5},{5,4},{6,7},{7,6},{8,9},{9,8},{10,11... | collective-permute-start | bytes 104 | tf_op jit(solution)/shard_map/ppermute | solution.py:58
  105.0 0.8 collective-permute-done.11
  105.8 5.6 %collective-permute-start.12 = (f32[8]{0:T(128)S(1)}, f32[8]{0:T(128)S(1)}, u32[]{:S(2)}, u32[]{:S(2)}) collective-permute-start(f32[8]{0:T(128)S(1)} %add.14), channel_id=1, source_target_pairs={{0,2},{1,3},{2,0},{3,1},{4,6},{5,7},{6,4},{7,5},{8,10},{9,11},{10,... | collective-permute-start | bytes 104 | tf_op jit(solution)/shard_map/ppermute | solution.py:58
  111.5 1.5 %collective-permute-done.12 = f32[8]{0:T(128)S(1)} collective-permute-done((f32[8]{0:T(128)S(1)}, f32[8]{0:T(128)S(1)}, u32[]{:S(2)}, u32[]{:S(2)}) %collective-permute-start.12) | collective-permute-done | bytes 64 | tf_op jit(solution)/shard_map/ppermute | solution.py:58
  113.0 3.7 %collective-permute-start.13 = (f32[8]{0:T(128)S(1)}, f32[8]{0:T(128)S(1)}, u32[]{:S(2)}, u32[]{:S(2)}) collective-permute-start(f32[8]{0:T(128)S(1)} %add.15), channel_id=1, source_target_pairs={{0,4},{1,5},{2,6},{3,7},{4,0},{5,1},{6,2},{7,3},{8,12},{9,13},{10,... | collective-permute-start | bytes 104 | tf_op jit(solution)/shard_map/ppermute | solution.py:58
  116.7 1.5 %collective-permute-done.13 = f32[8]{0:T(128)S(1)} collective-permute-done((f32[8]{0:T(128)S(1)}, f32[8]{0:T(128)S(1)}, u32[]{:S(2)}, u32[]{:S(2)}) %collective-permute-start.13) | collective-permute-done | bytes 64 | tf_op jit(solution)/shard_map/ppermute | solution.py:58
  118.3 7.7 %collective-permute-start.14 = (f32[8]{0:T(128)S(1)}, f32[8]{0:T(128)S(1)}, u32[]{:S(2)}, u32[]{:S(2)}) collective-permute-start(f32[8]{0:T(128)S(1)} %add.16), channel_id=1, source_target_pairs={{0,8},{1,9},{2,10},{3,11},{4,12},{5,13},{6,14},{7,15},{8,0},{9,1},... | collective-permute-start | bytes 104 | tf_op jit(solution)/shard_map/ppermute | solution.py:58
  125.9 1.5 %collective-permute-done.14 = f32[8]{0:T(128)S(1)} collective-permute-done((f32[8]{0:T(128)S(1)}, f32[8]{0:T(128)S(1)}, u32[]{:S(2)}, u32[]{:S(2)}) %collective-permute-start.14) | collective-permute-done | bytes 64 | tf_op jit(solution)/shard_map/ppermute | solution.py:58
  127.5 0.5 add.17
  (29 shorter events, 0.3 us)
Async XLA Ops:
  5.2 8.5 %copy-start.7 = (s32[256]{0:T(256)S(1)}, s32[256]{0:T(256)}, u32[]{:S(2)}) copy-start(s32[256]{0:T(256)} %param.10) | copy-start | bytes 3076
  5.2 74.2 %collective-permute-start.3 = (bf16[256,4096]{1,0:T(8,128)(2,1)}, bf16[256,4096]{1,0:T(8,128)(2,1)S(1)}, u32[]{:S(2)}, u32[]{:S(2)}) collective-permute-start(bf16[256,4096]{1,0:T(8,128)(2,1)} %get-tuple-element.20), channel_id=1, source_target_pairs={{0,1},{1,0},{2,3},{3,2},{4,5},{5,4},{6,7},{7,6},{8,9},{9,8},{10,11... | collective-permute-start | bytes 6291464 | tf_op jit(solution)/shard_map/ppermute | solution.py:43
  8.3 37.2 %collective-permute-start = (bf16[256,1024]{1,0:T(8,128)(2,1)}, bf16[256,1024]{1,0:T(8,128)(2,1)S(1)}, u32[]{:S(2)}, u32[]{:S(2)}) collective-permute-start(bf16[256,1024]{1,0:T(8,128)(2,1)} %get-tuple-element.16), channel_id=1, source_target_pairs={{1,2},{2,1},{3,4},{4,3},{5,6},{6,5},{7,8},{8,7},{9,10},{10,9},{11,... | collective-permute-start | bytes 1572872 | tf_op jit(solution)/shard_map/ppermute | solution.py:50
  9.0 36.6 %collective-permute-start.1 = (bf16[256,1024]{1,0:T(8,128)(2,1)}, bf16[256,1024]{1,0:T(8,128)(2,1)}, u32[]{:S(2)}, u32[]{:S(2)}) collective-permute-start(bf16[256,1024]{1,0:T(8,128)(2,1)} %get-tuple-element.17), channel_id=1, source_target_pairs={{0,1},{1,0},{2,3},{3,2},{4,5},{5,4},{6,7},{7,6},{8,9},{9,8},{10,11... | collective-permute-start | bytes 1572872 | tf_op jit(solution)/shard_map/ppermute | solution.py:43
  13.0 41.4 %collective-permute-start.10 = (bf16[256,1024]{1,0:T(8,128)(2,1)}, bf16[256,1024]{1,0:T(8,128)(2,1)S(1)}, u32[]{:S(2)}, u32[]{:S(2)}) collective-permute-start(bf16[256,1024]{1,0:T(8,128)(2,1)} %get-tuple-element.23), channel_id=1, source_target_pairs={{1,2},{2,1},{3,4},{4,3},{5,6},{6,5},{7,8},{8,7},{9,10},{10,9},{11,... | collective-permute-start | bytes 1572872 | tf_op jit(solution)/shard_map/ppermute | solution.py:50
  45.6 8.1 %copy-start.5 = (bf16[256,2048]{1,0:T(8,128)(2,1)S(1)}, bf16[256,2048]{1,0:T(8,128)(2,1)}, u32[]{:S(2)}) copy-start(bf16[256,2048]{1,0:T(8,128)(2,1)} %get-tuple-element.22) | copy-start | bytes 3145732
  45.6 31.9 %copy-start.6 = (bf16[256,1024]{1,0:T(8,128)(2,1)S(1)}, bf16[256,1024]{1,0:T(8,128)(2,1)}, u32[]{:S(2)}) copy-start(bf16[256,1024]{1,0:T(8,128)(2,1)} %get-tuple-element.19) | copy-start | bytes 1572868
  45.6 33.8 %copy-start.2 = (f32[4096]{0:T(1024)S(1)}, f32[4096]{0:T(1024)}, u32[]{:S(2)}) copy-start(f32[4096]{0:T(1024)} %param.11) | copy-start | bytes 49156
  45.6 33.8 %copy-start.3 = (s32[24]{0:T(128)S(1)}, s32[24]{0:T(128)}, u32[]{:S(2)}) copy-start(s32[24]{0:T(128)} %psum.7.info.refs_0_) | copy-start | bytes 292
  45.6 0.8 copy-start.4
  51.0 8.5 %collective-permute-start.5 = (bf16[256,1024]{1,0:T(8,128)(2,1)}, bf16[256,1024]{1,0:T(8,128)(2,1)S(1)}, u32[]{:S(2)}, u32[]{:S(2)}) collective-permute-start(bf16[256,1024]{1,0:T(8,128)(2,1)} %get-tuple-element.21.refs_5_), channel_id=1, source_target_pairs={{0,4},{1,5},{2,6},{3,7},{4,8},{5,9},{6,10},{7,11},{8,12},{9,13},{1... | collective-permute-start | bytes 1572872 | tf_op jit(solution)/shard_map/ppermute | solution.py:39
  52.4 25.1 %collective-permute-start.4 = (bf16[256,1024]{1,0:T(8,128)(2,1)}, bf16[256,1024]{1,0:T(8,128)(2,1)S(1)}, u32[]{:S(2)}, u32[]{:S(2)}) collective-permute-start(bf16[256,1024]{1,0:T(8,128)(2,1)} %get-tuple-element.21.refs_5_), channel_id=1, source_target_pairs={{0,2},{1,3},{2,4},{3,5},{4,6},{5,7},{6,8},{7,9},{8,10},{9,11},{10,... | collective-permute-start | bytes 1572872 | tf_op jit(solution)/shard_map/ppermute | solution.py:39
  53.7 31.9 %collective-permute-start.9 = (bf16[256,2048]{1,0:T(8,128)(2,1)S(1)}, bf16[256,2048]{1,0:T(8,128)(2,1)S(1)}, u32[]{:S(2)}, u32[]{:S(2)}) collective-permute-start(bf16[256,2048]{1,0:T(8,128)(2,1)S(1)} %copy-done.5), channel_id=1, source_target_pairs={{1,2},{2,1},{3,4},{4,3},{5,6},{6,5},{7,8},{8,7},{9,10},{10,9},{11,... | collective-permute-start | bytes 3145736 | tf_op jit(solution)/shard_map/ppermute | solution.py:50
  54.5 23.1 %collective-permute-start.6 = (bf16[256,1024]{1,0:T(8,128)(2,1)}, bf16[256,1024]{1,0:T(8,128)(2,1)S(1)}, u32[]{:S(2)}, u32[]{:S(2)}) collective-permute-start(bf16[256,1024]{1,0:T(8,128)(2,1)} %get-tuple-element.21.refs_5_), channel_id=1, source_target_pairs={{0,1},{2,3},{4,5},{6,7},{8,9},{10,11},{12,13},{14,15},{16,17},{18,... | collective-permute-start | bytes 1572872 | tf_op jit(solution)/shard_map/ppermute | solution.py:438
  59.5 18.7 %collective-permute-start.8 = (bf16[256,1024]{1,0:T(8,128)(2,1)S(1)}, bf16[256,1024]{1,0:T(8,128)(2,1)S(1)}, u32[]{:S(2)}, u32[]{:S(2)}) collective-permute-start(bf16[256,1024]{1,0:T(8,128)(2,1)S(1)} %collective-permute-done.5.refs_7_), channel_id=1, source_target_pairs={{1,0},{3,2},{5,4},{7,6},{9,8},{11,10},{13,12},{15,14},{17,16},{19,... | collective-permute-start | bytes 1572872 | tf_op jit(solution)/shard_map/ppermute | solution.py:446
  77.5 1.9 %collective-permute-start.7 = (bf16[256,1024]{1,0:T(8,128)(2,1)S(1)}, bf16[256,1024]{1,0:T(8,128)(2,1)S(1)}, u32[]{:S(2)}, u32[]{:S(2)}) collective-permute-start(bf16[256,1024]{1,0:T(8,128)(2,1)S(1)} %collective-permute-done.4.refs_6_), channel_id=1, source_target_pairs={{0,1},{1,0},{2,3},{3,2},{4,5},{5,4},{6,7},{7,6},{8,9},{9,8},{10,11... | collective-permute-start | bytes 1572872 | tf_op jit(solution)/shard_map/ppermute | solution.py:43
  77.5 13.6 %collective-permute-start.2 = (bf16[256,1024]{1,0:T(8,128)(2,1)S(1)}, bf16[256,1024]{1,0:T(8,128)(2,1)S(1)}, u32[]{:S(2)}, u32[]{:S(2)}) collective-permute-start(bf16[256,1024]{1,0:T(8,128)(2,1)S(1)} %copy-done.6), channel_id=1, source_target_pairs={{1,2},{2,1},{3,4},{4,3},{5,6},{6,5},{7,8},{8,7},{9,10},{10,9},{11,... | collective-permute-start | bytes 1572872 | tf_op jit(solution)/shard_map/ppermute | solution.py:50
  79.4 1.6 %copy-start = (bf16[256,4096]{1,0:T(8,128)(2,1)S(1)}, bf16[256,4096]{1,0:T(8,128)(2,1)}, u32[]{:S(2)}) copy-start(bf16[256,4096]{1,0:T(8,128)(2,1)} %get-tuple-element.18.refs_2_) | copy-start | bytes 6291460
  81.0 1.0 copy-start.1
  95.4 10.4 %collective-permute-start.11 = (f32[8]{0:T(128)S(1)}, f32[8]{0:T(128)S(1)}, u32[]{:S(2)}, u32[]{:S(2)}) collective-permute-start(f32[8]{0:T(128)S(1)} %reduce_sum.19), channel_id=1, source_target_pairs={{0,1},{1,0},{2,3},{3,2},{4,5},{5,4},{6,7},{7,6},{8,9},{9,8},{10,11... | collective-permute-start | bytes 104 | tf_op jit(solution)/shard_map/ppermute | solution.py:58
  105.8 7.2 %collective-permute-start.12 = (f32[8]{0:T(128)S(1)}, f32[8]{0:T(128)S(1)}, u32[]{:S(2)}, u32[]{:S(2)}) collective-permute-start(f32[8]{0:T(128)S(1)} %add.14), channel_id=1, source_target_pairs={{0,2},{1,3},{2,0},{3,1},{4,6},{5,7},{6,4},{7,5},{8,10},{9,11},{10,... | collective-permute-start | bytes 104 | tf_op jit(solution)/shard_map/ppermute | solution.py:58
  113.0 5.2 %collective-permute-start.13 = (f32[8]{0:T(128)S(1)}, f32[8]{0:T(128)S(1)}, u32[]{:S(2)}, u32[]{:S(2)}) collective-permute-start(f32[8]{0:T(128)S(1)} %add.15), channel_id=1, source_target_pairs={{0,4},{1,5},{2,6},{3,7},{4,0},{5,1},{6,2},{7,3},{8,12},{9,13},{10,... | collective-permute-start | bytes 104 | tf_op jit(solution)/shard_map/ppermute | solution.py:58
  118.3 9.2 %collective-permute-start.14 = (f32[8]{0:T(128)S(1)}, f32[8]{0:T(128)S(1)}, u32[]{:S(2)}, u32[]{:S(2)}) collective-permute-start(f32[8]{0:T(128)S(1)} %add.16), channel_id=1, source_target_pairs={{0,8},{1,9},{2,10},{3,11},{4,12},{5,13},{6,14},{7,15},{8,0},{9,1},... | collective-permute-start | bytes 104 | tf_op jit(solution)/shard_map/ppermute | solution.py:58

commit v3 on v2

--- a/solution.py
+++ b/solution.py
@@ -21,7 +21,7 @@
 WIDTH = HEADS * D_HEAD
 CHUNK = PER_GROUP * D_HEAD
 STACKED = PER_GROUP * BLOCK
-PAIR = 2
+PAIR = 4
 MASKED = -1e30
 WIDE = pltpu.CompilerParams(vmem_limit_bytes=58 * 1024 * 1024 + 256 * 1024)
 SLIM = pltpu.CompilerParams(vmem_limit_bytes=28 * 1024 * 1024)
@@ -55,8 +55,10 @@
         return lax.psum(part, "dp")
     bit = 1
     while bit < ranks:
-        part = part + lax.ppermute(part, "dp", [(i, i ^ bit) for i in range(ranks)])
-        bit *= 2
+        steps = [bit, 2 * bit, 3 * bit] if 2 * bit < ranks else [bit]
+        heard = [lax.ppermute(part, "dp", [(i, i ^ step) for i in range(ranks)]) for step in steps]
+        part = part + sum(heard)
+        bit *= 4
     return part
 
 
@@ -130,7 +132,7 @@
         in_specs=[SMEM, SMEM, HBM],
         out_specs=(VMEM,) * len(widths),
         scratch_shapes=[pltpu.SemaphoreType.DMA((len(SPLIT),))],
-        compiler_params=WIDE,
+        compiler_params=pltpu.CompilerParams(vmem_limit_bytes=48 * 1024 * 1024),
         name="second_stage",
     )(counts, place, queries)
 
@@ -200,7 +202,7 @@
         scratch_shapes=[
             pltpu.SemaphoreType.DMA((RECV, 3)),
         ],
-        compiler_params=WIDE,
+        compiler_params=pltpu.CompilerParams(vmem_limit_bytes=48 * 1024 * 1024),
         name="pack",
     )(info, place, queries, keys, values, outer, inner)
 

time: 128 us -> 125 us (0.977)
  Pallas kernels: 24.3 us -> 22.2 us
  waiting for transfers between devices: 23.3 us -> 22 us
  starting transfers between devices: 43 us -> 44.3 us
    pallas_call x1, Pallas kernels: 4.63 us -> 3.07 us  [pack(): pl.pallas_call(functools.partial(pack_kernel, responses, ranks, capacity)...]
    ppermute x4 -> x6, starting transfers between devices: 26.6 us -> 27.8 us  [total_over(): lax.ppermute(part, 'dp', [(i, i ^ step) for i in range(ranks)])]
    ppermute x4 -> x6, waiting for transfers between devices: 5.46 us -> 4.59 us  [total_over(): lax.ppermute(part, 'dp', [(i, i ^ step) for i in range(ranks)])]
  transfers between devices with their start and end apart: 15 -> 17, of which waited for: 6 -> 5; matrix products, arithmetic and copies ran while one was open for 0% -> 0% of each run, Pallas kernels for 13% -> 12%
where the time goes in v3:
time: 125 us
  starting transfers between devices  44.3 us (35%)
  blocking collectives  31.1 us (25%)
  Pallas kernels  22.2 us (18%)
  waiting for transfers between devices  22 us (18%)
  local copies, waits for them, and re-layouts  2.93 us (2%)
  between operations  1.48 us (1%)
    psum x1, blocking collectives, shards(): info = lax.psum(jnp.concatenate([smaller, marks]), 'dp')  31.1 us
    ppermute x6, starting transfers between devices, total_over(): lax.ppermute(part, 'dp', [(i, i ^ step) for i in range(ranks)])  27.8 us
    ppermute x2, waiting for transfers between devices, shifted(): return lax.ppermute(block, axis, route)  16.2 us
    pallas_call x3, Pallas kernels, attend(): pl.pallas_call(body, out_shape=out_shape, in_specs=in_specs, out_specs=[H...  13.1 us
    ppermute x1, starting transfers between devices, shards(): sib_own = lax.ppermute(own, 'dp', [(2 * m, 2 * m + 1) for m in pairs])  5.27 us
    ppermute x6, waiting for transfers between devices, total_over(): lax.ppermute(part, 'dp', [(i, i ^ step) for i in range(ranks)])  4.59 us
    ppermute x3, starting transfers between devices, inner_pairs(): return lax.ppermute(block, 'dp', [(i, i ^ 1) for i in range(ranks)])  3.72 us
    ppermute x4, starting transfers between devices, outer_pairs(): return lax.ppermute(block, 'dp', route)  3.57 us
  transfers between devices with their start and end apart: 17, of which 5 were waited for; matrix products, arithmetic and copies ran while one was open for 0% of the time, Pallas kernels for 12%

profile of v3, /device:TPU:0, one launch (start us, length us, event | category | flops | bytes accessed | tf_op | source)
XLA Modules:
  0.0 124.8 jit_solution(10575727429865873955)
XLA Ops:
  1.3 3.4 %second_stage.1 = (bf16[256,2048]{1,0:T(8,128)(2,1)S(1)}, bf16[256,1024]{1,0:T(8,128)(2,1)S(1)}, bf16[256,4096]{1,0:T(8,128)(2,1)}) custom-call(s32[1]{0:T(128)} %copy.12.counts, s32[1]{0:T(128)} %bitcast.1.place.refs_1_, bf16[768,4096]{1,0:T(8,128)(2,1)} %queries.5), custom_call_target="tpu_custom_call" | custom-call | tf_op jit(solution)/shard_map/second_stage/pallas_call | solution.py:129
  4.7 1.0 copy-done.3
  5.7 0.8 copy-done.5
  6.5 0.5 collective-permute-start.3
  7.0 2.5 %first_stage.1 = (bf16[256,1024]{1,0:T(8,128)(2,1)}, bf16[256,1024]{1,0:T(8,128)(2,1)}, bf16[256,1024]{1,0:T(8,128)(2,1)}) custom-call(s32[1]{0:T(128)} %copy.12.counts, s32[1]{0:T(128)} %bitcast.1.place.refs_1_, bf16[768,4096]{1,0:T(8,128)(2,1)} %queries.5, bf16[768,512]{1,0:T(8,128)(2,1)} %keys.3, bf16[768,512]{1,0:T(8,128)(2,1)} %values.3), custom_call_target="tpu_custom_call" | custom-call | tf_op jit(solution)/shard_map/first_stage/pallas_call | solution.py:104
  9.6 1.5 %collective-permute-start = (bf16[256,1024]{1,0:T(8,128)(2,1)}, bf16[256,1024]{1,0:T(8,128)(2,1)}, u32[]{:S(2)}, u32[]{:S(2)}) collective-permute-start(bf16[256,1024]{1,0:T(8,128)(2,1)} %get-tuple-element.16), channel_id=1, source_target_pairs={{1,2},{2,1},{3,4},{4,3},{5,6},{6,5},{7,8},{8,7},{9,10},{10,9},{11,... | collective-permute-start | bytes 1572872 | tf_op jit(solution)/shard_map/ppermute | solution.py:50
  11.0 3.2 %collective-permute-start.1 = (bf16[256,1024]{1,0:T(8,128)(2,1)}, bf16[256,1024]{1,0:T(8,128)(2,1)}, u32[]{:S(2)}, u32[]{:S(2)}) collective-permute-start(bf16[256,1024]{1,0:T(8,128)(2,1)} %get-tuple-element.17), channel_id=1, source_target_pairs={{0,1},{1,0},{2,3},{3,2},{4,5},{5,4},{6,7},{7,6},{8,9},{9,8},{10,11... | collective-permute-start | bytes 1572872 | tf_op jit(solution)/shard_map/ppermute | solution.py:43
  14.3 0.7 collective-permute-start.10
  15.2 31.1 %psum.7.info.refs_0_ = s32[24]{0:T(128)S(1)} all-reduce(s32[24]{0:T(128)S(1)} %pad_add_fusion), channel_id=1, replica_groups=mesh['groups'=2,'dp'=16] {'dp'}, use_global_device_ids=true, to_apply=%region_1.2 | all-reduce | flops 24 | bytes 192 | tf_op jit(solution)/shard_map/psum | solution.py:434
  46.3 1.1 copy-done.1
  47.4 3.1 %pack.1 = (bf16[256,1024]{1,0:T(8,128)(2,1)S(1)}, bf16[256,4096]{1,0:T(8,128)(2,1)S(1)}) custom-call(s32[24]{0:T(128)S(1)} %psum.7.info.refs_0_, s32[1]{0:T(128)} %bitcast.1.place.refs_1_, bf16[768,4096]{1,0:T(8,128)(2,1)} %queries.5, bf16[768,512]{1,0:T(8,128)(2,1)S(1)} %copy-done, bf16[768,512]{1,0:T(8,128)(2,1)S(1)} %copy-done.1, ...), custom_call_target="tpu_custom_call" | custom-call | tf_op jit(solution)/shard_map/pack/pallas_call | solution.py:194
  50.5 1.3 %collective-permute-start.5 = (bf16[256,1024]{1,0:T(8,128)(2,1)S(1)}, bf16[256,1024]{1,0:T(8,128)(2,1)S(1)}, u32[]{:S(2)}, u32[]{:S(2)}) collective-permute-start(bf16[256,1024]{1,0:T(8,128)(2,1)S(1)} %get-tuple-element.21.refs_5_), channel_id=1, source_target_pairs={{0,4},{1,5},{2,6},{3,7},{4,8},{5,9},{6,10},{7,11},{8,12},{9,13},{1... | collective-permute-start | bytes 1572872 | tf_op jit(solution)/shard_map/ppermute | solution.py:39
  51.8 1.3 %collective-permute-start.4 = (bf16[256,1024]{1,0:T(8,128)(2,1)S(1)}, bf16[256,1024]{1,0:T(8,128)(2,1)S(1)}, u32[]{:S(2)}, u32[]{:S(2)}) collective-permute-start(bf16[256,1024]{1,0:T(8,128)(2,1)S(1)} %get-tuple-element.21.refs_5_), channel_id=1, source_target_pairs={{0,2},{1,3},{2,4},{3,5},{4,6},{5,7},{6,8},{7,9},{8,10},{9,11},{10,... | collective-permute-start | bytes 1572872 | tf_op jit(solution)/shard_map/ppermute | solution.py:39
  53.2 0.7 collective-permute-start.9
  53.9 5.3 %collective-permute-start.6 = (bf16[256,1024]{1,0:T(8,128)(2,1)S(1)}, bf16[256,1024]{1,0:T(8,128)(2,1)S(1)}, u32[]{:S(2)}, u32[]{:S(2)}) collective-permute-start(bf16[256,1024]{1,0:T(8,128)(2,1)S(1)} %get-tuple-element.21.refs_5_), channel_id=1, source_target_pairs={{0,1},{2,3},{4,5},{6,7},{8,9},{10,11},{12,13},{14,15},{16,17},{18,... | collective-permute-start | bytes 1572872 | tf_op jit(solution)/shard_map/ppermute | solution.py:440
  59.2 1.3 %collective-permute-start.8 = (bf16[256,1024]{1,0:T(8,128)(2,1)S(1)}, bf16[256,1024]{1,0:T(8,128)(2,1)S(1)}, u32[]{:S(2)}, u32[]{:S(2)}) collective-permute-start(bf16[256,1024]{1,0:T(8,128)(2,1)S(1)} %collective-permute-done.5.refs_7_), channel_id=1, source_target_pairs={{1,0},{3,2},{5,4},{7,6},{9,8},{11,10},{13,12},{15,14},{17,16},{19,... | collective-permute-start | bytes 1572872 | tf_op jit(solution)/shard_map/ppermute | solution.py:448
  60.5 16.2 %collective-permute-done.4.refs_6_ = bf16[256,1024]{1,0:T(8,128)(2,1)S(1)} collective-permute-done((bf16[256,1024]{1,0:T(8,128)(2,1)S(1)}, bf16[256,1024]{1,0:T(8,128)(2,1)S(1)}, u32[]{:S(2)}, u32[]{:S(2)}) %collective-permute-start.4) | collective-permute-done | bytes 524320 | tf_op jit(solution)/shard_map/ppermute | solution.py:39
  76.7 0.7 collective-permute-start.2
  77.4 1.2 collective-permute-done.7.refs_9_
  78.6 3.5 %shard_map.77 = (bf16[256,4096]{1,0:T(8,128)(2,1)}, f32[256,128]{1,0:T(8,128)S(1)}) custom-call(s32[24]{0:T(128)S(1)} %psum.7.info.refs_0_, s32[1]{0:T(128)} %bitcast.1.place.refs_1_, bf16[256,4096]{1,0:T(8,128)(2,1)S(1)} %get-tuple-element.18.refs_2_, bf16[256,1024]{1,0:T(8,128)(2,1)S(1)} %collective-permute-done.10.refs_3_, ...), custom_call_target="tpu_custom_call" | custom-call | flops 1342177280 | bytes 2097152 | tf_op jit(solution)/shard_map/pallas_call | solution.py:393
  82.1 5.4 %shard_map.78 = (bf16[256,4096]{1,0:T(8,128)(2,1)}, f32[256,128]{1,0:T(8,128)S(1)}) custom-call(s32[24]{0:T(128)S(1)} %psum.7.info.refs_0_, s32[1]{0:T(128)} %bitcast.1.place.refs_1_, bf16[256,4096]{1,0:T(8,128)(2,1)S(1)} %get-tuple-element.18.refs_2_, bf16[256,2048]{1,0:T(8,128)(2,1)S(1)} %collective-permute-done.9.refs_3_, ...), custom_call_target="tpu_custom_call", output_to_operand_aliasing={{0}: (12, {})} | custom-call | flops 2684354560 | bytes 4194304 | tf_op jit(solution)/shard_map/pallas_call | solution.py:393
  87.6 4.2 %shard_map.79 = (bf16[256,4096]{1,0:T(8,128)(2,1)}, f32[256,128]{1,0:T(8,128)}, f32[8,128]{1,0:T(8,128)S(1)}) custom-call(s32[24]{0:T(128)S(1)} %psum.7.info.refs_0_, s32[1]{0:T(128)} %bitcast.1.place.refs_1_, bf16[256,4096]{1,0:T(8,128)(2,1)S(1)} %get-tuple-element.18.refs_2_, ...), custom_call_target="tpu_custom_call", output_to_operand_aliasing={{0}: (12, {})} | custom-call | flops 1342177280 | bytes 2097152 | tf_op jit(solution)/shard_map/pallas_call | solution.py:393
  91.8 0.1 reduce_sum.19
  91.9 6.6 %collective-permute-start.13 = (f32[8]{0:T(128)S(1)}, f32[8]{0:T(128)S(1)}, u32[]{:S(2)}, u32[]{:S(2)}) collective-permute-start(f32[8]{0:T(128)S(1)} %reduce_sum.19), channel_id=1, source_target_pairs={{0,3},{1,2},{2,1},{3,0},{4,7},{5,6},{6,5},{7,4},{8,11},{9,10},{10,... | collective-permute-start | bytes 104 | tf_op jit(solution)/shard_map/ppermute | solution.py:59
  98.4 11.3 %collective-permute-start.12 = (f32[8]{0:T(128)S(1)}, f32[8]{0:T(128)S(1)}, u32[]{:S(2)}, u32[]{:S(2)}) collective-permute-start(f32[8]{0:T(128)S(1)} %reduce_sum.19), channel_id=1, source_target_pairs={{0,2},{1,3},{2,0},{3,1},{4,6},{5,7},{6,4},{7,5},{8,10},{9,11},{10,... | collective-permute-start | bytes 104 | tf_op jit(solution)/shard_map/ppermute | solution.py:59
  109.8 1.5 %collective-permute-done.12 = f32[8]{0:T(128)S(1)} collective-permute-done((f32[8]{0:T(128)S(1)}, f32[8]{0:T(128)S(1)}, u32[]{:S(2)}, u32[]{:S(2)}) %collective-permute-start.12) | collective-permute-done | bytes 64 | tf_op jit(solution)/shard_map/ppermute | solution.py:59
  111.3 1.2 collective-permute-start.16
  112.6 8.2 %collective-permute-start.15 = (f32[8]{0:T(128)S(1)}, f32[8]{0:T(128)S(1)}, u32[]{:S(2)}, u32[]{:S(2)}) collective-permute-start(f32[8]{0:T(128)S(1)} %add_add_fusion.1), channel_id=1, source_target_pairs={{0,8},{1,9},{2,10},{3,11},{4,12},{5,13},{6,14},{7,15},{8,0},{9,1},... | collective-permute-start | bytes 104 | tf_op jit(solution)/shard_map/ppermute | solution.py:59
  120.7 0.5 collective-permute-start.14
  121.2 1.1 collective-permute-done.15
  122.3 2.0 %collective-permute-done.14 = f32[8]{0:T(128)S(1)} collective-permute-done((f32[8]{0:T(128)S(1)}, f32[8]{0:T(128)S(1)}, u32[]{:S(2)}, u32[]{:S(2)}) %collective-permute-start.14) | collective-permute-done | bytes 64 | tf_op jit(solution)/shard_map/ppermute | solution.py:59
  124.3 0.5 add_add_fusion
  (31 shorter events, 0.3 us)
Async XLA Ops:
  4.7 1.0 copy-start.3
  5.7 0.8 copy-start.5
  6.5 8.4 %copy-start.7 = (s32[256]{0:T(256)S(1)}, s32[256]{0:T(256)}, u32[]{:S(2)}) copy-start(s32[256]{0:T(256)} %param.10) | copy-start | bytes 3076
  6.5 39.8 %copy-start = (bf16[768,512]{1,0:T(8,128)(2,1)S(1)}, bf16[768,512]{1,0:T(8,128)(2,1)}, u32[]{:S(2)}) copy-start(bf16[768,512]{1,0:T(8,128)(2,1)} %keys.3) | copy-start | bytes 2359300
  6.5 72.1 %collective-permute-start.3 = (bf16[256,4096]{1,0:T(8,128)(2,1)}, bf16[256,4096]{1,0:T(8,128)(2,1)S(1)}, u32[]{:S(2)}, u32[]{:S(2)}) collective-permute-start(bf16[256,4096]{1,0:T(8,128)(2,1)} %get-tuple-element.20), channel_id=1, source_target_pairs={{0,1},{1,0},{2,3},{3,2},{4,5},{5,4},{6,7},{7,6},{8,9},{9,8},{10,11... | collective-permute-start | bytes 6291464 | tf_op jit(solution)/shard_map/ppermute | solution.py:43
  9.6 36.7 %collective-permute-start = (bf16[256,1024]{1,0:T(8,128)(2,1)}, bf16[256,1024]{1,0:T(8,128)(2,1)}, u32[]{:S(2)}, u32[]{:S(2)}) collective-permute-start(bf16[256,1024]{1,0:T(8,128)(2,1)} %get-tuple-element.16), channel_id=1, source_target_pairs={{1,2},{2,1},{3,4},{4,3},{5,6},{6,5},{7,8},{8,7},{9,10},{10,9},{11,... | collective-permute-start | bytes 1572872 | tf_op jit(solution)/shard_map/ppermute | solution.py:50
  11.0 35.2 %collective-permute-start.1 = (bf16[256,1024]{1,0:T(8,128)(2,1)}, bf16[256,1024]{1,0:T(8,128)(2,1)}, u32[]{:S(2)}, u32[]{:S(2)}) collective-permute-start(bf16[256,1024]{1,0:T(8,128)(2,1)} %get-tuple-element.17), channel_id=1, source_target_pairs={{0,1},{1,0},{2,3},{3,2},{4,5},{5,4},{6,7},{7,6},{8,9},{9,8},{10,11... | collective-permute-start | bytes 1572872 | tf_op jit(solution)/shard_map/ppermute | solution.py:43
  14.3 39.7 %collective-permute-start.10 = (bf16[256,1024]{1,0:T(8,128)(2,1)}, bf16[256,1024]{1,0:T(8,128)(2,1)S(1)}, u32[]{:S(2)}, u32[]{:S(2)}) collective-permute-start(bf16[256,1024]{1,0:T(8,128)(2,1)} %get-tuple-element.23), channel_id=1, source_target_pairs={{1,2},{2,1},{3,4},{4,3},{5,6},{6,5},{7,8},{8,7},{9,10},{10,9},{11,... | collective-permute-start | bytes 1572872 | tf_op jit(solution)/shard_map/ppermute | solution.py:50
  46.3 1.1 copy-start.1
  47.4 5.8 %copy-start.4 = (bf16[256,2048]{1,0:T(8,128)(2,1)S(1)}, bf16[256,2048]{1,0:T(8,128)(2,1)}, u32[]{:S(2)}) copy-start(bf16[256,2048]{1,0:T(8,128)(2,1)} %copy-done.3) | copy-start | bytes 3145732
  47.4 29.3 %copy-start.6 = (bf16[256,1024]{1,0:T(8,128)(2,1)S(1)}, bf16[256,1024]{1,0:T(8,128)(2,1)}, u32[]{:S(2)}) copy-start(bf16[256,1024]{1,0:T(8,128)(2,1)} %copy-done.5) | copy-start | bytes 1572868
  47.4 31.2 %copy-start.2 = (f32[4096]{0:T(1024)S(1)}, f32[4096]{0:T(1024)}, u32[]{:S(2)}) copy-start(f32[4096]{0:T(1024)} %param.11) | copy-start | bytes 49156
  50.5 8.7 %collective-permute-start.5 = (bf16[256,1024]{1,0:T(8,128)(2,1)S(1)}, bf16[256,1024]{1,0:T(8,128)(2,1)S(1)}, u32[]{:S(2)}, u32[]{:S(2)}) collective-permute-start(bf16[256,1024]{1,0:T(8,128)(2,1)S(1)} %get-tuple-element.21.refs_5_), channel_id=1, source_target_pairs={{0,4},{1,5},{2,6},{3,7},{4,8},{5,9},{6,10},{7,11},{8,12},{9,13},{1... | collective-permute-start | bytes 1572872 | tf_op jit(solution)/shard_map/ppermute | solution.py:39
  51.8 24.8 %collective-permute-start.4 = (bf16[256,1024]{1,0:T(8,128)(2,1)S(1)}, bf16[256,1024]{1,0:T(8,128)(2,1)S(1)}, u32[]{:S(2)}, u32[]{:S(2)}) collective-permute-start(bf16[256,1024]{1,0:T(8,128)(2,1)S(1)} %get-tuple-element.21.refs_5_), channel_id=1, source_target_pairs={{0,2},{1,3},{2,4},{3,5},{4,6},{5,7},{6,8},{7,9},{8,10},{9,11},{10,... | collective-permute-start | bytes 1572872 | tf_op jit(solution)/shard_map/ppermute | solution.py:39
  53.2 28.9 %collective-permute-start.9 = (bf16[256,2048]{1,0:T(8,128)(2,1)S(1)}, bf16[256,2048]{1,0:T(8,128)(2,1)S(1)}, u32[]{:S(2)}, u32[]{:S(2)}) collective-permute-start(bf16[256,2048]{1,0:T(8,128)(2,1)S(1)} %copy-done.4), channel_id=1, source_target_pairs={{1,2},{2,1},{3,4},{4,3},{5,6},{6,5},{7,8},{8,7},{9,10},{10,9},{11,... | collective-permute-start | bytes 3145736 | tf_op jit(solution)/shard_map/ppermute | solution.py:50
  53.9 22.7 %collective-permute-start.6 = (bf16[256,1024]{1,0:T(8,128)(2,1)S(1)}, bf16[256,1024]{1,0:T(8,128)(2,1)S(1)}, u32[]{:S(2)}, u32[]{:S(2)}) collective-permute-start(bf16[256,1024]{1,0:T(8,128)(2,1)S(1)} %get-tuple-element.21.refs_5_), channel_id=1, source_target_pairs={{0,1},{2,3},{4,5},{6,7},{8,9},{10,11},{12,13},{14,15},{16,17},{18,... | collective-permute-start | bytes 1572872 | tf_op jit(solution)/shard_map/ppermute | solution.py:440
  59.2 18.2 %collective-permute-start.8 = (bf16[256,1024]{1,0:T(8,128)(2,1)S(1)}, bf16[256,1024]{1,0:T(8,128)(2,1)S(1)}, u32[]{:S(2)}, u32[]{:S(2)}) collective-permute-start(bf16[256,1024]{1,0:T(8,128)(2,1)S(1)} %collective-permute-done.5.refs_7_), channel_id=1, source_target_pairs={{1,0},{3,2},{5,4},{7,6},{9,8},{11,10},{13,12},{15,14},{17,16},{19,... | collective-permute-start | bytes 1572872 | tf_op jit(solution)/shard_map/ppermute | solution.py:448
  76.7 1.9 %collective-permute-start.7 = (bf16[256,1024]{1,0:T(8,128)(2,1)S(1)}, bf16[256,1024]{1,0:T(8,128)(2,1)S(1)}, u32[]{:S(2)}, u32[]{:S(2)}) collective-permute-start(bf16[256,1024]{1,0:T(8,128)(2,1)S(1)} %collective-permute-done.4.refs_6_), channel_id=1, source_target_pairs={{0,1},{1,0},{2,3},{3,2},{4,5},{5,4},{6,7},{7,6},{8,9},{9,8},{10,11... | collective-permute-start | bytes 1572872 | tf_op jit(solution)/shard_map/ppermute | solution.py:43
  76.7 10.9 %collective-permute-start.2 = (bf16[256,1024]{1,0:T(8,128)(2,1)S(1)}, bf16[256,1024]{1,0:T(8,128)(2,1)S(1)}, u32[]{:S(2)}, u32[]{:S(2)}) collective-permute-start(bf16[256,1024]{1,0:T(8,128)(2,1)S(1)} %copy-done.6), channel_id=1, source_target_pairs={{1,2},{2,1},{3,4},{4,3},{5,6},{6,5},{7,8},{8,7},{9,10},{10,9},{11,... | collective-permute-start | bytes 1572872 | tf_op jit(solution)/shard_map/ppermute | solution.py:50
  91.9 17.9 %collective-permute-start.13 = (f32[8]{0:T(128)S(1)}, f32[8]{0:T(128)S(1)}, u32[]{:S(2)}, u32[]{:S(2)}) collective-permute-start(f32[8]{0:T(128)S(1)} %reduce_sum.19), channel_id=1, source_target_pairs={{0,3},{1,2},{2,1},{3,0},{4,7},{5,6},{6,5},{7,4},{8,11},{9,10},{10,... | collective-permute-start | bytes 104 | tf_op jit(solution)/shard_map/ppermute | solution.py:59
  98.4 12.9 %collective-permute-start.12 = (f32[8]{0:T(128)S(1)}, f32[8]{0:T(128)S(1)}, u32[]{:S(2)}, u32[]{:S(2)}) collective-permute-start(f32[8]{0:T(128)S(1)} %reduce_sum.19), channel_id=1, source_target_pairs={{0,2},{1,3},{2,0},{3,1},{4,6},{5,7},{6,4},{7,5},{8,10},{9,11},{10,... | collective-permute-start | bytes 104 | tf_op jit(solution)/shard_map/ppermute | solution.py:59
  109.8 1.6 %collective-permute-start.11 = (f32[8]{0:T(128)S(1)}, f32[8]{0:T(128)S(1)}, u32[]{:S(2)}, u32[]{:S(2)}) collective-permute-start(f32[8]{0:T(128)S(1)} %reduce_sum.19), channel_id=1, source_target_pairs={{0,1},{1,0},{2,3},{3,2},{4,5},{5,4},{6,7},{7,6},{8,9},{9,8},{10,11... | collective-permute-start | bytes 104 | tf_op jit(solution)/shard_map/ppermute | solution.py:59
  111.3 9.9 %collective-permute-start.16 = (f32[8]{0:T(128)S(1)}, f32[8]{0:T(128)S(1)}, u32[]{:S(2)}, u32[]{:S(2)}) collective-permute-start(f32[8]{0:T(128)S(1)} %add_add_fusion.1), channel_id=1, source_target_pairs={{0,12},{1,13},{2,14},{3,15},{4,8},{5,9},{6,10},{7,11},{8,4},{9,5},... | collective-permute-start | bytes 104 | tf_op jit(solution)/shard_map/ppermute | solution.py:59
  112.6 9.7 %collective-permute-start.15 = (f32[8]{0:T(128)S(1)}, f32[8]{0:T(128)S(1)}, u32[]{:S(2)}, u32[]{:S(2)}) collective-permute-start(f32[8]{0:T(128)S(1)} %add_add_fusion.1), channel_id=1, source_target_pairs={{0,8},{1,9},{2,10},{3,11},{4,12},{5,13},{6,14},{7,15},{8,0},{9,1},... | collective-permute-start | bytes 104 | tf_op jit(solution)/shard_map/ppermute | solution.py:59
  120.7 3.6 %collective-permute-start.14 = (f32[8]{0:T(128)S(1)}, f32[8]{0:T(128)S(1)}, u32[]{:S(2)}, u32[]{:S(2)}) collective-permute-start(f32[8]{0:T(128)S(1)} %add_add_fusion.1), channel_id=1, source_target_pairs={{0,4},{1,5},{2,6},{3,7},{4,0},{5,1},{6,2},{7,3},{8,12},{9,13},{10,... | collective-permute-start | bytes 104 | tf_op jit(solution)/shard_map/ppermute | solution.py:59
